TPU v7x, 256 devices: a whole 4x4x8 slice. The times are simulated.
256 devices in a mesh: row: 4 (over x_hi, core), col: 4 (over y), depth: 16 (over z, x_lo).
Axes of the slice: x: 4 (x_hi: 2, x_lo: 2; x = x_hi * 2 + x_lo), y: 4, z: 8, core: 2. Of those that a mesh axis runs over, the one named last changes fastest.
Arguments:
- acts: bfloat16 [2048, 32768], P('depth', 'row'), may hold values from -6 to 6
- act_mask: int32 [2048, 256], P('depth', 'row'), may hold values 0 or 1
- w1: bfloat16 [256, 32, 128, 128], P(('row', 'depth'), 'col'), may hold values from -0.09375 to 0.09375
- cols1: int32 [256, 32], P('row', 'col'), may hold values from 0 to 255, as said below
- bias1: float32 [32768], P('col'), may hold values from -3 to 3
- mask2: int32 [2048, 256], P('depth', 'col'), may hold values 0 or 1
- w2: bfloat16 [256, 32, 128, 128], P(('col', 'depth'), 'row'), may hold values from -0.1875 to 0.1875
- cols2: int32 [256, 32], P('col', 'row'), may hold values from 0 to 255, as said below
- bias2: float32 [32768], P(('row', 'col')), may hold values from -3 to 3
Outputs:
- result: bfloat16 [2048, 32768], P('depth', ('row', 'col'))
Inputs may be any that keep to these rules, and one draw needn't show every extreme that they name: `cols1`: in each of the 256 block rows the 32 entries name different block columns, and for every g the entries g * 8 to g * 8 + 7 lie among block columns g * 64 to g * 64 + 63. `cols2`: in each of the 256 block rows the 32 entries name different block columns, and for every g the entries g * 8 to g * 8 + 7 lie among block columns g * 64 to g * 64 + 63.
All inputs are finite; a program needn't handle non-finite values. No bound on the sum of `act_mask` or of `mask2` on one device may be relied on, other than what follows from the above.
Results may differ from a plain program's by a relative error of at most 0.0047.
Values may be sent and summed in bfloat16 or wider, within the bound.
A program may use at most 128 MiB of HBM per device.

v0:
```python
import jax
import jax.numpy as jnp
from jax import lax
from jax.sharding import Mesh
from jax.sharding import PartitionSpec as P

DEPTH = ("depth_0", "depth_1")
ROW_DEPTH = ("row", "depth_0", "depth_1")
COL_DEPTH = ("col", "depth_0", "depth_1")


def whole_of(x, axes, dim):
    result = x
    for number in range(len(axes) - 1, -1, -1):
        result = lax.all_gather(result, axes[number], axis=dim, tiled=True)
    return result


def split_up(x, dim, count):
    lengths = x.shape
    parts = x.reshape(*lengths[:dim], count, lengths[dim] // count, *lengths[dim + 1 :])
    return jnp.moveaxis(parts, dim, 0)


def summed_on_arrival(x, axis, dim):
    count = lax.axis_size(axis)
    parts = lax.all_to_all(split_up(x, dim, count), axis, 0, 0, tiled=True)
    return jnp.sum(parts, axis=0)


def sent_to_all(x, axis):
    count = lax.axis_size(axis)
    return lax.all_to_all(jnp.broadcast_to(x[None], (count, *x.shape)), axis, 0, 0, tiled=True)


def in_order(parts, dim):
    lengths = list(parts.shape[1:])
    lengths[dim] *= parts.shape[0]
    return jnp.moveaxis(parts, 0, dim).reshape(lengths)


def collect(x, axis, dim):
    parts = sent_to_all(x, axis)
    return in_order(parts, dim)


def fold_function(inputs, targets, stride):

    def add_tiles(running_total, tiles, first_row):

        def advance(number, total):
            offset = number * stride
            block_list = lax.dynamic_slice_in_dim(tiles, offset, stride, 0)
            incoming_rows = lax.dynamic_slice_in_dim(inputs, offset, stride, 1)
            wanted = lax.dynamic_slice_in_dim(targets, offset, stride, 0)
            product = jnp.einsum(
                "tws,wish->twih", incoming_rows, block_list, preferred_element_type=jnp.float32
            )
            flat_product = product.reshape(product.shape[0], -1, product.shape[-1])
            return total.at[:, wanted.reshape(-1)].add(flat_product)

        return lax.fori_loop(0, tiles.shape[0] // stride, advance, running_total)

    return add_tiles


def on_device(acts, act_mask, w1, cols1, bias1, mask2, w2, cols2, bias2):
    block = w1.shape[-1]
    rows_dev = acts.shape[0]
    row_blocks = act_mask.shape[1]
    col_blocks = mask2.shape[1]
    row_index = lax.axis_index("row")
    col_index = lax.axis_index("col")
    masked = acts.reshape(rows_dev, row_blocks, block) * act_mask[:, :, None].astype(jnp.bfloat16)
    first_layer_destinations = cols1 - col_index * col_blocks
    second_targets = cols2 - row_index * row_blocks
    first_offset_value = jnp.zeros((rows_dev, col_blocks, block), jnp.float32)
    first_fold = fold_function(masked, first_layer_destinations, w1.shape[0])
    first_sum = first_fold(first_offset_value, whole_of(w1, DEPTH, 0), jnp.int32(0))
    bias_blocks = bias1.reshape(col_blocks, block)
    share = col_blocks // lax.axis_size("row")
    part_sum = summed_on_arrival(first_sum, "row", 1)
    bias_part = lax.dynamic_slice_in_dim(bias_blocks, row_index * share, share, 0)
    mask_part = lax.dynamic_slice_in_dim(mask2, row_index * share, share, 1)
    hidden_part = jnp.maximum(part_sum + bias_part, 0.0) * mask_part[:, :, None].astype(jnp.float32)
    hidden = collect(hidden_part.astype(jnp.bfloat16), "row", 1)
    second_start = jnp.zeros((rows_dev, row_blocks, block), jnp.float32)
    second_fold = fold_function(hidden, second_targets, w2.shape[0])
    second_sum = second_fold(
        second_start, lax.all_gather(w2, DEPTH, axis=0, tiled=True), jnp.int32(0)
    )
    outcome = summed_on_arrival(second_sum, "col", 1)
    bias_out = bias2.reshape(outcome.shape[1], block)
    return jnp.maximum(outcome + bias_out, 0.0).astype(jnp.bfloat16).reshape(rows_dev, -1)


def solution(mesh):
    finer = Mesh(
        mesh.devices.reshape(mesh.shape["row"], mesh.shape["col"], 8, 2),
        ("row", "col", "depth_0", "depth_1"),
    )
    in_specs = (
        P(DEPTH, "row"),
        P(DEPTH, "row"),
        P(ROW_DEPTH, "col", None, None),
        P("row", "col"),
        P("col"),
        P(DEPTH, "col"),
        P(COL_DEPTH, "row", None, None),
        P("col", "row"),
        P(("row", "col")),
    )
    out_specs = P(DEPTH, ("row", "col"))
    return jax.shard_map(
        on_device, mesh=finer, in_specs=in_specs, out_specs=out_specs, check_vma=False
    )
```

profile of v0, /device:TPU:1, one launch (start us, length us, event | category | flops | bytes accessed | tf_op | source)
XLA Modules:
  0.0 895.9 jit_solution(4881494235092866972)
XLA Ops:
  7.3 43.6 %all-gather.6.cloned.1.call-done = bf16[8,8,128,128]{3,2,1,0:T(8,128)(2,1)} async-done(((bf16[4,8,128,128]{3,2,1,0:T(8,128)(2,1)}), bf16[8,8,128,128]{3,2,1,0:T(8,128)(2,1)}) %all-gather.6.cloned.1.call-update) | async-done | bytes 2097168 | tf_op jit(solution)/shard_map/all_gather | solution.py:15
  51.8 3.2 copy.36
  56.5 170.0 %all-gather.8.cloned.1.call-done = bf16[64,8,128,128]{3,2,1,0:T(8,128)(2,1)} async-done(((bf16[8,8,128,128]{3,2,1,0:T(8,128)(2,1)}), bf16[64,8,128,128]{3,2,1,0:T(8,128)(2,1)}) %all-gather.8.cloned.1.call-update) | async-done | bytes 16777232 | tf_op jit(solution)/shard_map/all_gather | solution.py:15
  229.1 182.0 %while.26 = (s32[]{:T(128)}, f32[128,64,128]{2,0,1:T(8,128)}, s32[64,8]{1,0:T(8,128)S(1)}, bf16[64,8,128,128]{3,2,1,0:T(8,128)(2,1)}, bf16[128,64,128]{0,2,1:T(8...) while((s32[]{:T(128)}, f32[128,64,128]{2,0,1:T(8,128)}, s32[64,8]{1,0:T(8,128)S(1)}, ...), condition=%wide.region_2.0_spmd, body=%wide.region_0.0_spmd.sunk | while | flops 134742112 | bytes 13764623 | solution.py:62
  234.2 6.3 scatter_fusion
  245.6 6.2 scatter_fusion
  256.9 6.3 scatter_fusion
  268.4 6.3 scatter_fusion
  279.8 6.2 scatter_fusion
  291.2 6.2 scatter_fusion
  302.5 6.3 scatter_fusion
  314.0 6.2 scatter_fusion
  325.3 6.3 scatter_fusion
  336.7 6.3 scatter_fusion
  348.1 6.2 scatter_fusion
  359.5 6.3 scatter_fusion
  370.9 6.3 scatter_fusion
  382.3 6.2 scatter_fusion
  393.6 6.2 scatter_fusion
  404.9 6.2 scatter_fusion
  411.1 5.7 all-to-all-start
  417.4 141.3 %all-to-all-done = f32[4,128,16,128]{3,1,2,0:T(8,128)} async-done(((f32[4,128,16,128]{3,1,2,0:T(8,128)}), f32[4,128,16,128]{3,1,2,0:T(8,128)}, u32[]{:S(2)}, u32[]{:S(2)}) %all-to-all-start) | async-done | bytes 4194336 | tf_op jit(solution)/shard_map/all_to_all | solution.py:27
  563.6 5.4 all-to-all-start.1
  569.1 76.2 %all-gather.4.cloned.1.call-done = bf16[64,8,128,128]{3,2,1,0:T(8,128)(2,1)} async-done(((bf16[4,8,128,128]{3,2,1,0:T(8,128)(2,1)}), bf16[64,8,128,128]{3,2,1,0:T(8,128)(2,1)}) %all-gather.4.cloned.1.call-update) | async-done | bytes 16777232 | tf_op jit(solution)/shard_map/all_gather | solution.py:90
  648.6 181.9 %while.27 = (s32[]{:T(128)}, f32[128,64,128]{2,0,1:T(8,128)}, s32[64,8]{1,0:T(8,128)S(1)}, bf16[64,8,128,128]{3,2,1,0:T(8,128)(2,1)}, bf16[128,64,128]{2,0,1:T(8...) while((s32[]{:T(128)}, f32[128,64,128]{2,0,1:T(8,128)}, s32[64,8]{1,0:T(8,128)S(1)}, ...), condition=%wide.region_6.0_spmd, body=%wide.region_4.0_spmd.sunk | while | flops 134742112 | bytes 13764623 | solution.py:62
  648.6 3.1 fusion.29
  653.8 6.2 scatter_fusion.1
  665.2 6.2 scatter_fusion.1
  671.4 3.1 fusion.29
  676.5 6.2 scatter_fusion.1
  687.9 6.2 scatter_fusion.1
  699.2 6.2 scatter_fusion.1
  710.6 6.2 scatter_fusion.1
  716.7 3.1 fusion.29
  721.9 6.2 scatter_fusion.1
  728.1 3.1 fusion.29
  733.3 6.2 scatter_fusion.1
  744.6 6.2 scatter_fusion.1
  750.9 3.1 fusion.29
  756.0 6.2 scatter_fusion.1
  762.2 3.1 fusion.29
  767.4 6.3 scatter_fusion.1
  778.8 6.2 scatter_fusion.1
  790.1 6.2 scatter_fusion.1
  801.5 6.2 scatter_fusion.1
  812.9 6.3 scatter_fusion.1
  824.3 6.3 scatter_fusion.1
  830.5 54.2 %all_to_all.15 = f32[4,128,16,128]{3,1,2,0:T(8,128)} all-to-all(f32[4,128,16,128]{3,1,2,0:T(8,128)} %bitcast.62), channel_id=1, replica_groups=mesh['row'=4,'col'=4,'depth_0'=8,'depth_1'=2] {'col'}, dimensions={0} | all-to-all | bytes 8388608 | tf_op jit(solution)/shard_map/all_to_all | solution.py:27
  (190 shorter events, 164.5 us)
Async XLA Ops:
  6.5 410.2 %copy-start = (f32[8192]{0:T(1024)S(1)}, f32[8192]{0:T(1024)}, u32[]{:S(2)}) copy-start(f32[8192]{0:T(1024)} %param.17) | copy-start | bytes 98308
  6.5 45.2 %copy-start.4 = (s32[64,8]{0,1:T(8,128)S(1)}, s32[64,8]{0,1:T(8,128)}, u32[]{:S(2)}) copy-start(s32[64,8]{0,1:T(8,128)} %param.16) | copy-start | bytes 6148
  6.5 44.4 %all-gather.6.cloned.1.call-start = ((), (), s32[]{:S(2)}) async-start(), calls=%async_computation.4 | async-start | bytes 3145728 | tf_op jit(solution)/shard_map/all_gather | solution.py:15
  7.3 219.2 %all-gather.8.cloned.1.call-start = ((), (), s32[]{:S(2)}) async-start(), calls=%async_computation.5 | async-start | bytes 18874368 | tf_op jit(solution)/shard_map/all_gather | solution.py:15
  51.0 594.3 %all-gather.4.cloned.1.call-start = ((), (), s32[]{:S(2)}) async-start(), calls=%async_computation.3 | async-start | bytes 17825792 | tf_op jit(solution)/shard_map/all_gather | solution.py:90
  51.8 3.2 copy-start.2
  411.1 147.7 %all-to-all-start = ((f32[4,128,16,128]{3,1,2,0:T(8,128)}), f32[4,128,16,128]{3,1,2,0:T(8,128)}, u32[]{:S(2)}, u32[]{:S(2)}) async-start(f32[4,128,16,128]{3,1,2,0:T(8,128)} %bitcast.61), calls=%async_computation | async-start | bytes 8388608 | tf_op jit(solution)/shard_map/all_to_all | solution.py:27
  563.6 5.4 copy-start.5
  563.6 82.6 %all-to-all-start.1 = ((bf16[4,128,16,128]{3,1,2,0:T(8,128)(2,1)}), bf16[4,128,16,128]{3,1,2,0:T(8,128)(2,1)}, u32[]{:S(2)}, u32[]{:S(2)}) async-start(bf16[4,128,16,128]{3,1,2,0:T(8,128)(2,1)} %broadcast_in_dim.7), calls=%async_computation.1 | async-start | bytes 4194304 | tf_op jit(solution)/shard_map/all_to_all | solution.py:33
  884.7 4.7 copy-start.1
  887.4 0.7 copy-start.3
Sparse Core Ops, SparseCore 0:
  9.1 41.7 all-gather.5
  52.7 173.7 all-gather.7
  228.3 416.9 all-gather.3
where the time goes:
time: 907 us; the launch traced here: 896 us
  waiting for transfers between devices  433 us (48%)
  other arithmetic  208 us (23%)
  matrix products  99.2 us (11%)
  local copies, waits for them, and re-layouts  76.5 us (8%)
  blocking collectives  54.2 us (6%)
  between operations  13.2 us (1%)
  starting transfers between devices  11.1 us (1%)
    all_gather x2, waiting for transfers between devices, whole_of(): result = lax.all_gather(result, axes[number], axis=dim, tiled=True)  214 us
    scatter-add x32, other arithmetic, advance(): return total.at[:, wanted.reshape(-1)].add(flat_product)  199 us
    all_to_all x1, waiting for transfers between devices, summed_on_arrival(): parts = lax.all_to_all(split_up(x, dim, count), axis, 0, 0, tiled=True)  141 us
    dot_general x32, matrix products, advance(): jnp.einsum('tws,wish->twih', incoming_rows, block_list, preferred_element...  99.2 us
    all_gather x1, waiting for transfers between devices, on_device(): lax.all_gather(w2, DEPTH, axis=0, tiled=True)  76.2 us
    reshape x32, local copies, waits for them, and re-layouts, advance(): flat_product = product.reshape(product.shape[0], -1, product.shape[-1])  61.5 us
    all_to_all x1, blocking collectives, summed_on_arrival(): parts = lax.all_to_all(split_up(x, dim, count), axis, 0, 0, tiled=True)  54.2 us
  transfers between devices with their start and end apart: 5, of which 5 were waited for; matrix products, arithmetic and copies ran while one was open for 22% of the time, Pallas kernels for 0%

commit v1 on v0

v1 whole, which is shorter than its diff:
```python
import functools

import jax
import jax.numpy as jnp
from jax import lax
from jax.experimental import pallas as pl
from jax.experimental.pallas import tpu as pltpu
from jax.sharding import Mesh
from jax.sharding import PartitionSpec as P

AXES = ("xh", "core", "y", "z", "xl")
DEPTH = ("z", "xl")
ROW = ("xh", "core")
SWAP = ((0, 0), (1, 2), (2, 1), (3, 3))
BF16, F32 = jnp.bfloat16, jnp.float32


def flip(i):
    return i + 1 - 2 * lax.rem(i, 2)


def xor4(i, j):
    low = lax.rem(i + j, 2)
    high = lax.rem(i // 2 + j // 2, 2)
    return high * 2 + low


def product_kernel(load, store, rows_in_step, pos_ref, core_ref, x_ref, w_ref, keep_ref, send_ref, acc_ref):
    step = pl.program_id(0)
    columns, entries = acc_ref.shape[0], w_ref.shape[1]

    @pl.when(step == 0)
    def _():
        @pl.loop(0, columns)
        def _(c):
            acc_ref[c] = jnp.zeros(acc_ref.shape[1:], F32)

    for b in range(rows_in_step):
        i = step * rows_in_step + b
        lhs = load(x_ref, i)
        for k in range(0, entries, 2):
            rhs = jnp.concatenate([w_ref[b, k], w_ref[b, k + 1]], axis=1)
            out = jnp.dot(lhs, rhs, preferred_element_type=F32)
            width = out.shape[1] // 2
            acc_ref[pos_ref[i, k]] += out[:, :width]
            acc_ref[pos_ref[i, k + 1]] += out[:, width:]

    @pl.when(step == pl.num_programs(0) - 1)
    def _():
        store(core_ref[0], acc_ref, keep_ref, send_ref)


def store_columns(core, acc_ref, keep_ref, send_ref):
    half = keep_ref.shape[0]

    @pl.loop(0, half)
    def _(c):
        keep_ref[c] = acc_ref[c]
        send_ref[c] = acc_ref[c + half].astype(BF16)


def store_rows(core, acc_ref, keep_ref, send_ref):
    rows = keep_ref.shape[1]
    mine = pl.multiple_of(core * rows, rows)
    theirs = pl.multiple_of((1 - core) * rows, rows)

    @pl.loop(0, keep_ref.shape[0])
    def _(c):
        keep_ref[c] = acc_ref[c, pl.ds(mine, rows), :]
        send_ref[c] = acc_ref[c, pl.ds(theirs, rows), :].astype(BF16)


def load_columns(x_ref, i):
    return x_ref[:, pl.ds(pl.multiple_of(i * 128, 128), 128)]


def load_blocks(x_ref, i):
    return x_ref[i]


def products(x, w, pos, core, load, store, out_shape, rows, columns, name):
    block_rows, entries, bs, _ = w.shape
    rows_in_step = 4
    whole = lambda shape: pl.BlockSpec(shape, lambda s, *_: (0,) * len(shape))
    return pl.pallas_call(
        functools.partial(product_kernel, load, store, rows_in_step),
        out_shape=(jax.ShapeDtypeStruct(out_shape, F32), jax.ShapeDtypeStruct(out_shape, BF16)),
        grid_spec=pltpu.PrefetchScalarGridSpec(
            num_scalar_prefetch=2,
            grid=(block_rows // rows_in_step,),
            in_specs=[
                whole(x.shape),
                pl.BlockSpec((rows_in_step, entries, bs, bs), lambda s, *_: (s, 0, 0, 0)),
            ],
            out_specs=[whole(out_shape), whole(out_shape)],
            scratch_shapes=[pltpu.VMEM((columns, rows, bs), F32)],
        ),
        compiler_params=pltpu.CompilerParams(vmem_limit_bytes=48 << 20),
        cost_estimate=pl.CostEstimate(
            flops=2 * rows * block_rows * entries * bs * bs,
            bytes_accessed=w.size * 2 + x.size * 2 + 6 * out_shape[0] * out_shape[1] * bs,
            transcendentals=0,
        ),
        name=name,
    )(pos, core, x, w)


def remote(src, dst, sems, n, device):
    return pltpu.make_async_remote_copy(
        src_ref=src,
        dst_ref=dst,
        send_sem=sems.at[0, n],
        recv_sem=sems.at[1, n],
        device_id=device,
        device_id_type=pl.DeviceIdType.MESH,
    )


def greet(devices):
    barrier = pltpu.get_barrier_semaphore()
    for device in devices:
        pl.semaphore_signal(barrier, inc=1, device_id=device, device_id_type=pl.DeviceIdType.MESH)
    pl.semaphore_wait(barrier, len(devices))


FIRST = ((2, 1), (2, 3))
LANDS = ((3, 0), (1, 0))


def reduce_scatter(other, near, keep, send, got, out1, in1, out2, in2, sems, finish):
    half = keep.shape[1] // 2

    def part(ref, g, h):
        return ref.at[g, pl.ds(h * half, half)]

    exchanged = {}
    order = [(2, 0), (2, 1), (1, 0), (3, 1), (3, 0), (1, 1), (0, 0), (0, 1)]
    for n, (g, h) in enumerate(order):
        exchanged[g, h] = remote(part(send, g, h), part(got, g, h), sems, n, other)
        exchanged[g, h].start()

    def both(g, h, c):
        return keep[g, h * half + c] + got[g, h * half + c].astype(F32)

    firsts = {}
    for s in range(2):
        for h in range(2):
            g = FIRST[h][s]
            exchanged[g, h].wait_recv()

            @pl.loop(0, half)
            def _(c):
                out1[h, s, c] = both(g, h, c).astype(BF16)

            firsts[h, s] = remote(out1.at[h, s], in1.at[h, s], sems, 8 + 2 * h + s, near[h])
            firsts[h, s].start()
    seconds = {}
    for h in range(2):
        g = LANDS[h][0]
        exchanged[g, h].wait_recv()
        firsts[h, 0].wait_recv()

        @pl.loop(0, half)
        def _(c):
            out2[h, c] = (both(g, h, c) + in1[h, 0, c].astype(F32)).astype(BF16)

        seconds[h] = remote(out2.at[h], in2.at[h], sems, 12 + h, near[1 - h])
        seconds[h].start()
    for h in range(2):
        exchanged[0, h].wait_recv()
        firsts[h, 1].wait_recv()
        seconds[h].wait_recv()
        finish(h, lambda c: both(0, h, c) + in1[h, 1, c].astype(F32) + in2[h, c].astype(F32))
    for copy in [*exchanged.values(), *firsts.values(), *seconds.values()]:
        copy.wait_send()


def hidden_kernel(keep, send, bias, mask, hid, got, out1, in1, out2, in2, sems):
    xh, core, xl = lax.axis_index("xh"), lax.axis_index("core"), lax.axis_index("xl")
    x = xh * 2 + xl
    other = {"core": 1 - core}
    near = ({"xl": 1 - xl}, {"xh": 1 - xh, "xl": 1 - xl})
    index = (flip(x), 3 - x)
    greet((other, *near))
    half = keep.shape[1] // 2

    def piece(chip, h):
        return hid.at[chip, pl.ds(h * half, half)]

    copies = []

    def spread(chip, h, to, n):
        copy = remote(piece(chip, h), piece(chip, h), sems, n, near[to])
        copy.start()
        copies.append(copy)
        return copy

    given = {}

    def finish(h, total):
        for c in range(half):
            n = h * half + c
            value = jnp.maximum(total(c) + bias[pl.ds(n, 1), :], 0.0) * mask[n].astype(F32)
            hid[x, n] = value.astype(BF16)
        for to in (1 - h, h):
            given[h, to] = spread(x, h, to, 14 + 2 * h + to)

    reduce_scatter(other, near, keep, send, got, out1, in1, out2, in2, sems, finish)
    for h in range(2):
        given[h, 1 - h].wait_recv()
        spread(index[1 - h], h, h, 18 + h)
    for h in range(2):
        given[h, h].wait_recv()
    for copy in copies[4:]:
        copy.wait_recv()
    for copy in copies:
        copy.wait_send()


def result_kernel(keep, send, bias, out, got, out1, in1, out2, in2, fin, sems):
    core, y, xl = lax.axis_index("core"), lax.axis_index("y"), lax.axis_index("xl")
    other = {"core": 1 - core}
    near = ({"y": flip(y)}, {"y": 3 - y})
    home = {"core": 1 - core, "xl": 1 - xl}
    away = xl != core
    greet((other, *near, home))
    half = keep.shape[1] // 2
    bs = keep.shape[-1]

    def back(h):
        piece = pl.ds(h * half * bs, half * bs)
        return remote(fin.at[:, piece], out.at[:, piece], sems, 14 + h, home)

    def finish(h, total):
        for c in range(half):
            n = h * half + c
            value = jnp.maximum(total(c) + bias[pl.ds(n, 1), :], 0.0)
            fin[:, n * bs : (n + 1) * bs] = value.astype(BF16)

        @pl.when(away)
        def _():
            back(h).start()

    reduce_scatter(other, near, keep, send, got, out1, in1, out2, in2, sems, finish)

    @pl.when(away)
    def _():
        for h in range(2):
            back(h).wait()

    @pl.when(jnp.logical_not(away))
    def _():
        out[...] = fin[...]


def summed(kernel, keep, send, operands, out_shape, extra, n_sems, collective_id, name):
    chips, blocks, rows, bs = keep.shape
    half = (blocks // 2, rows, bs)
    vmem = pl.BlockSpec(memory_space=pltpu.VMEM)
    return pl.pallas_call(
        kernel,
        out_shape=jax.ShapeDtypeStruct(out_shape, BF16),
        in_specs=[vmem] * (2 + len(operands)),
        out_specs=vmem,
        scratch_shapes=[
            pltpu.VMEM(keep.shape, BF16),
            pltpu.VMEM((2, 2, *half), BF16),
            pltpu.VMEM((2, 2, *half), BF16),
            pltpu.VMEM((2, *half), BF16),
            pltpu.VMEM((2, *half), BF16),
            *extra,
            pltpu.SemaphoreType.DMA((2, n_sems)),
        ],
        compiler_params=pltpu.CompilerParams(
            collective_id=collective_id, has_side_effects=True, vmem_limit_bytes=40 << 20
        ),
        cost_estimate=pl.CostEstimate(
            flops=40_000_000, bytes_accessed=40 << 20, transcendentals=0
        ),
        name=name,
    )(keep, send, *operands)


def on_device(acts, act_mask, w1, cols1, bias1, mask2, w2, cols2, bias2):
    bs = w1.shape[-1]
    rows = acts.shape[0]
    blocks = act_mask.shape[1]
    xh, core, y, xl = (lax.axis_index(a) for a in ("xh", "core", "y", "xl"))
    x = xh * 2 + xl

    w1_all = lax.all_gather(w1, "z", axis=0, tiled=True)
    w2_swapped = lax.ppermute(w2, ("core", "xl"), SWAP)
    w2_all = lax.all_gather(w2_swapped, "z", axis=0, tiled=True)
    cols2 = lax.ppermute(cols2, ("core", "xl"), SWAP)
    bias2 = lax.ppermute(bias2, ("core", "xl"), SWAP)

    live = jnp.repeat(act_mask.astype(BF16), bs, axis=1)
    masked = (acts * live).reshape(rows, 8, 2, 4 * bs)
    mine = lax.dynamic_index_in_dim(masked, xl, 2, keepdims=False).reshape(rows, -1)
    given = lax.dynamic_index_in_dim(masked, 1 - xl, 2, keepdims=False).reshape(rows, -1)
    taken = lax.ppermute(given, "xl", ((0, 1), (1, 0)))
    x0 = jnp.concatenate([jnp.where(xl == 0, mine, taken), jnp.where(xl == 0, taken, mine)], axis=0)

    near1 = lax.dynamic_index_in_dim(cols1.reshape(8, 2, 4, 8), xl, 1, keepdims=False).reshape(32, 8) - y * blocks
    chip1 = near1 // 16
    core1 = lax.rem(near1 // 4, 2)
    block1 = lax.rem(near1 // 8, 2) * 4 + lax.rem(near1, 4)
    pos1 = lax.rem(core1 + core, 2) * 32 + xor4(chip1, x) * 8 + block1
    me = core.astype(jnp.int32).reshape(1)
    keep1, send1 = products(
        x0, w1_all, pos1, me, load_columns, store_columns, (blocks // 2, 2 * rows, bs), 2 * rows, blocks, "layer1"
    )

    live2 = mask2.astype(BF16)
    live2_taken = lax.ppermute(live2, "xl", ((0, 1), (1, 0)))
    live2 = jnp.concatenate(
        [jnp.where(xl == 0, live2, live2_taken), jnp.where(xl == 0, live2_taken, live2)], axis=0
    ).reshape(2 * rows, 4, 2, 2, 4)
    live2 = lax.dynamic_index_in_dim(live2, x, 1, keepdims=False)
    live2 = lax.dynamic_index_in_dim(live2, core, 2, keepdims=False).reshape(2 * rows, 8)
    live2 = jnp.broadcast_to(live2.T[:, :, None], (8, 2 * rows, bs))
    part1 = lax.dynamic_index_in_dim(bias1.reshape(4, 2, 2, 4, bs), x, 0, keepdims=False)
    part1 = lax.dynamic_index_in_dim(part1, core, 1, keepdims=False).reshape(8, bs)
    shape1 = (4, 8, 2 * rows, bs)
    hidden = summed(
        hidden_kernel, keep1.reshape(shape1), send1.reshape(shape1), (part1, live2), shape1, (), 20, 0, "hidden"
    )

    near2 = lax.dynamic_index_in_dim(cols2.reshape(8, 2, 4, 8), core, 1, keepdims=False).reshape(32, 8) - x * blocks
    pos2 = xor4(near2 // 16, y) * 16 + lax.rem(near2, 16)
    keep2, send2 = products(
        hidden.reshape(32, 2 * rows, bs), w2_all, pos2, me, load_blocks, store_rows,
        (blocks, rows, bs), 2 * rows, blocks, "layer2",
    )
    shape2 = (4, 16, rows, bs)
    return summed(
        result_kernel, keep2.reshape(shape2), send2.reshape(shape2), (bias2.reshape(16, bs),),
        (rows, 16 * bs), (pltpu.VMEM((rows, 16 * bs), BF16),), 16, 1, "result",
    )


def solution(mesh):
    finer = Mesh(mesh.devices.reshape(2, 2, mesh.shape["col"], 8, 2), AXES)
    in_specs = (
        P(DEPTH, ROW),
        P(DEPTH, ROW),
        P((*ROW, *DEPTH), "y", None, None),
        P(ROW, "y"),
        P("y"),
        P(DEPTH, "y"),
        P(("y", *DEPTH), ROW, None, None),
        P("y", ROW),
        P((*ROW, "y")),
    )
    out_specs = P(DEPTH, (*ROW, "y"))
    return jax.shard_map(on_device, mesh=finer, in_specs=in_specs, out_specs=out_specs, check_vma=False)
```

time: 907 us -> 258 us (0.28); the launches traced: 896 us -> 257 us
  waiting for transfers between devices: 433 us -> 96 us
  other arithmetic: 208 us -> 3.1 us
  Pallas kernels: 0 us -> 104 us
  matrix products: 99.2 us -> 0 us
  blocking collectives: 54.2 us -> 0 us
  local copies, waits for them, and re-layouts: 76.5 us -> 28.6 us
    all_gather x3 -> x2, waiting for transfers between devices: 290 us -> 64.8 us  [the longest x1 34.3 us: on_device(): w2_all = lax.all_gather(w2_swapped, 'z', axis=0, tiled=True)]
    scatter-add x32 -> x0, other arithmetic: 199 us -> none  [advance(): return total.at[:, wanted.reshape(-1)].add(flat_product)]
    all_to_all x2 -> x0, waiting for transfers between devices: 142 us -> none  [the longest x1 141 us: summed_on_arrival(): parts = lax.all_to_all(split_up(x, dim, count), axis, 0, 0, tiled=True)]
    pallas_call x0 -> x4, Pallas kernels: none -> 104 us  [the longest x2 76.8 us: summed(): pl.pallas_call(kernel, out_shape=jax.ShapeDtypeStruct(out_shape, BF16), i...]
    dot_general x32 -> x0, matrix products: 99.2 us -> none  [advance(): jnp.einsum('tws,wish->twih', incoming_rows, block_list, preferred_element...]
    reshape x64 -> x3, local copies, waits for them, and re-layouts: 64.1 us -> 3.51 us  [the longest x1 3.49 us: on_device(): masked = (acts * live).reshape(rows, 8, 2, 4 * bs)]
    all_to_all x1 -> x0, blocking collectives: 54.2 us -> none  [summed_on_arrival(): parts = lax.all_to_all(split_up(x, dim, count), axis, 0, 0, tiled=True)]
    ppermute x0 -> x5, waiting for transfers between devices: none -> 30.5 us  [the longest x1 17.8 us: on_device(): cols2 = lax.ppermute(cols2, ('core', 'xl'), SWAP)]
  transfers between devices with their start and end apart: 5 -> 7, of which waited for: 5 -> 4; matrix products, arithmetic and copies ran while one was open for 22% -> 10% of each run, Pallas kernels for 0% -> 28%
where the time goes in v1:
time: 258 us; the launch traced here: 257 us
  Pallas kernels  104 us (40%)
  waiting for transfers between devices  96 us (37%)
  local copies, waits for them, and re-layouts  28.6 us (11%)
  between operations  13.7 us (5%)
  starting transfers between devices  12.2 us (5%)
  other arithmetic  3.1 us (1%)
    pallas_call x2, Pallas kernels, summed(): pl.pallas_call(kernel, out_shape=jax.ShapeDtypeStruct(out_shape, BF16), i...  76.8 us
    all_gather x1, waiting for transfers between devices, on_device(): w2_all = lax.all_gather(w2_swapped, 'z', axis=0, tiled=True)  34.3 us
    all_gather x1, waiting for transfers between devices, on_device(): w1_all = lax.all_gather(w1, 'z', axis=0, tiled=True)  30.4 us
    pallas_call x2, Pallas kernels, products(): pl.pallas_call(functools.partial(product_kernel, load, store, rows_in_ste...  26.8 us
    ppermute x1, waiting for transfers between devices, on_device(): cols2 = lax.ppermute(cols2, ('core', 'xl'), SWAP)  17.8 us
    dynamic_slice x1, local copies, waits for them, and re-layouts, on_device(): lax.dynamic_index_in_dim(masked, xl, 2, keepdims=False).reshape(rows, -1)  13.7 us
    ppermute x1, waiting for transfers between devices, on_device(): w2_swapped = lax.ppermute(w2, ('core', 'xl'), SWAP)  12.7 us
    unnamed x25, local copies, waits for them, and re-layouts  9.37 us
  transfers between devices with their start and end apart: 7, of which 4 were waited for; matrix products, arithmetic and copies ran while one was open for 10% of the time, Pallas kernels for 28%

profile of v1, /device:TPU:1, one launch (start us, length us, event | category | flops | bytes accessed | tf_op | source)
XLA Modules:
  0.0 257.2 jit_solution(1668968322828349342)
XLA Ops:
  6.5 0.0 copy-start
  6.5 0.0 copy-start.6
  6.5 0.0 copy-start.3
  6.5 0.0 all-gather.3.cloned.1.call-start
  6.5 0.7 all-gather.3.cloned.1.call-update
  7.3 0.0 all-gather.5.cloned.1.call-start
  7.3 4.5 %collective-permute-start.3 = (bf16[4,8,128,128]{3,2,1,0:T(8,128)(2,1)}, bf16[4,8,128,128]{3,2,1,0:T(8,128)(2,1)S(1)}, u32[]{:S(2)}, u32[]{:S(2)}) collective-permute-start(bf16[4,8,128,128]{3,2,1,0:T(8,128)(2,1)} %param.15), channel_id=1, source_target_pairs={{0,0},{1,64},{64,1},{65,65},{2,2},{3,66},{66,3},{67,67},{4,4},{5,6... | collective-permute-start | bytes 3145736 | tf_op jit(solution)/shard_map/ppermute | solution.py:292
  11.8 12.7 %collective-permute-done.3 = bf16[4,8,128,128]{3,2,1,0:T(8,128)(2,1)S(1)} collective-permute-done((bf16[4,8,128,128]{3,2,1,0:T(8,128)(2,1)}, bf16[4,8,128,128]{3,2,1,0:T(8,128)(2,1)S(1)}, u32[]{:S(2)}, u32[]{:S(2)}) %collective-permute-start.3) | collective-permute-done | bytes 1048608 | tf_op jit(solution)/shard_map/ppermute | solution.py:292
  24.5 1.0 copy-done.4
  25.5 0.0 all-gather.5.cloned.1.call-update
  25.5 0.0 copy-done.6
  25.5 0.1 copy.22
  25.6 1.6 broadcast_in_dim.4
  27.3 0.0 copy-done.3
  27.3 2.6 %bitcast_multiply_fusion = bf16[128,8192]{1,0:T(8,128)(2,1)} fusion(bf16[128,8192]{1,0:T(8,128)(2,1)S(1)} %copy-done.3, bf16[16,8,64,128]{3,2,1,0:T(8,128)(2,1)S(1)} %bitcast.33), kind=kLoop, calls=%fused_computation | loop fusion | flops 1048576 | bytes 6291456 | tf_op jit(solution)/shard_map/mul | solution.py:298
  29.9 3.5 %reshape.72 = bf16[128,8,2,512]{3,2,1,0:T(2,128)(2,1)S(1)} reshape(bf16[128,8192]{1,0:T(8,128)(2,1)} %bitcast_multiply_fusion) | data formatting | bytes 4194304 | tf_op jit(solution)/shard_map/reshape | solution.py:298
  33.4 13.7 %dynamic-slice_reduce_fusion.1 = (bf16[128,8,512]{2,1,0:T(8,128)(2,1)S(1)}, bf16[128,8,512]{2,1,0:T(8,128)(2,1)}) fusion(bf16[128,8,2,512]{3,2,1,0:T(2,128)(2,1)S(1)} %reshape.72, s32[]{:T(128)S(6)} %select_n.82, s32[]{:T(128)S(6)} %select_n.89), kind=kLoop, calls=%fused_computation.3 | loop fusion | bytes 4194312 | tf_op jit(solution)/shard_map/jit(dynamic_index_in_dim)/dynamic_slice | solution.py:299
  47.1 2.6 %copy.29 = bf16[16,8,8,512]{3,1,2,0:T(8,128)(2,1)} copy(bf16[16,8,8,512]{3,2,1,0:T(8,128)(2,1)} %bitcast.36) | data formatting | bytes 2097152
  49.7 0.0 collective-permute-start.1
  49.7 0.0 copy-done.5
  49.7 1.5 collective-permute-start.2
  51.2 0.0 copy-done.7
  51.2 0.1 copy.20
  51.3 4.2 %collective-permute-start = (s32[64,8]{1,0:T(8,128)S(1)}, s32[64,8]{1,0:T(8,128)S(1)}, u32[]{:S(2)}, u32[]{:S(2)}) collective-permute-start(s32[64,8]{1,0:T(8,128)S(1)} %copy.20), channel_id=1, source_target_pairs={{0,0},{1,64},{64,1},{65,65},{2,2},{3,66},{66,3},{67,67},{4,4},{5,6... | collective-permute-start | bytes 6152 | tf_op jit(solution)/shard_map/ppermute | solution.py:294
  55.5 0.0 copy-done.9
  55.5 1.9 collective-permute-start.4
  57.5 0.0 copy-done.8
  57.5 0.1 copy.21
  57.6 0.1 fusion.19.pos_ref
  57.7 0.0 copy-done
  57.7 0.4 copy.28
  58.1 17.8 %collective-permute-done = s32[64,8]{1,0:T(8,128)S(1)} collective-permute-done((s32[64,8]{1,0:T(8,128)S(1)}, s32[64,8]{1,0:T(8,128)S(1)}, u32[]{:S(2)}, u32[]{:S(2)}) %collective-permute-start) | collective-permute-done | bytes 2080 | tf_op jit(solution)/shard_map/ppermute | solution.py:294
  75.9 0.0 collective-permute-done.2
  76.0 0.0 collective-permute-done.1
  76.0 0.1 broadcast_select_fusion.1
  76.2 0.2 pad_maximum_fusion.x_ref
  76.4 30.4 %all-gather.3.cloned.1.call-done.w_ref = bf16[32,8,128,128]{3,2,1,0:T(8,128)(2,1)} async-done(((bf16[4,8,128,128]{3,2,1,0:T(8,128)(2,1)}), bf16[32,8,128,128]{3,2,1,0:T(8,128)(2,1)}) %all-gather.3.cloned.1.call-update) | async-done | bytes 8388624 | tf_op jit(solution)/shard_map/all_gather | solution.py:291
  106.9 13.3 %layer1.1 = (f32[32,256,128]{2,1,0:T(8,128)}, bf16[32,256,128]{2,1,0:T(8,128)(2,1)S(1)}) custom-call(s32[32,8]{1,0:T(8,128)S(1)} %fusion.19.pos_ref, s32[1]{0:T(128)} %bitcast.2.core_ref, bf16[256,4096]{1,0:T(8,128)(2,1)S(1)} %pad_maximum_fusion.x_ref, bf16[32,8,128,128]{3,2,1,0:T(8,128)(2,1)} %all-gather.3.cloned.1.call-done.w_ref), custom_call_target="tpu_custom_call" | custom-call | flops 2147483648 | bytes 16777216 | tf_op jit(solution)/shard_map/layer1/pallas_call | solution.py:85
  120.2 0.3 broadcast_in_dim.10.mask
  120.5 0.0 copy-start.2
  120.5 2.2 copy-done.2
  122.7 44.3 %hidden.1 = bf16[4,8,256,128]{3,2,1,0:T(8,128)(2,1)S(1)} custom-call(f32[4,8,256,128]{3,2,1,0:T(8,128)S(1)} %bitcast.28, bf16[4,8,256,128]{3,2,1,0:T(8,128)(2,1)S(1)} %bitcast.30, f32[8,128]{1,0:T(8,128)S(1)} %bitcast.31, bf16[8,256,128]{2,1,0:T(8,128)(2,1)S(1)} %broadcast_in_dim.10.mask), custom_call_target="tpu_custom_call" | custom-call | flops 40000000 | bytes 41943040 | tf_op jit(solution)/shard_map/hidden/pallas_call | solution.py:260
  167.0 34.3 %all-gather.5.cloned.1.call-done.w_ref = bf16[32,8,128,128]{3,2,1,0:T(8,128)(2,1)} async-done(((bf16[4,8,128,128]{3,2,1,0:T(8,128)(2,1)}), bf16[32,8,128,128]{3,2,1,0:T(8,128)(2,1)}) %all-gather.5.cloned.1.call-update) | async-done | bytes 8388624 | tf_op jit(solution)/shard_map/all_gather | solution.py:293
  201.4 13.5 %layer2.1 = (f32[64,128,128]{2,1,0:T(8,128)}, bf16[64,128,128]{2,1,0:T(8,128)(2,1)S(1)}) custom-call(s32[32,8]{1,0:T(8,128)S(1)} %fusion.6.pos_ref, s32[1]{0:T(128)} %bitcast.2.core_ref, bf16[32,256,128]{2,1,0:T(8,128)(2,1)S(1)} %bitcast.26, bf16[32,8,128,128]{3,2,1,0:T(8,128)(2,1)} %all-gather.5.cloned.1.call-done.w_ref), custom_call_target="tpu_custom_call" | custom-call | flops 2147483648 | bytes 16777216 | tf_op jit(solution)/shard_map/layer2/pallas_call | solution.py:85
  214.9 0.0 collective-permute-done.4
  214.9 2.2 copy-done.1
  217.1 32.5 %result.1 = bf16[128,2048]{1,0:T(8,128)(2,1)S(1)} custom-call(f32[4,16,128,128]{3,2,1,0:T(8,128)S(1)} %bitcast.27, bf16[4,16,128,128]{3,2,1,0:T(8,128)(2,1)S(1)} %bitcast.29, f32[16,128]{1,0:T(8,128)S(1)} %bitcast.32), custom_call_target="tpu_custom_call" | custom-call | flops 40000000 | bytes 41943040 | tf_op jit(solution)/shard_map/result/pallas_call | solution.py:260
  249.6 0.8 copy.32
  (17 shorter events, 0.1 us)
Async XLA Ops:
  6.5 51.1 %copy-start = (f32[8192]{0:T(1024)S(1)}, f32[8192]{0:T(1024)}, u32[]{:S(2)}) copy-start(f32[8192]{0:T(1024)} %param.13) | copy-start | bytes 98308
  6.5 19.0 %copy-start.6 = (s32[128,64]{0,1:T(8,128)S(1)}, s32[128,64]{0,1:T(8,128)}, u32[]{:S(2)}) copy-start(s32[128,64]{0,1:T(8,128)} %param.10) | copy-start | bytes 98308
  6.5 20.7 %copy-start.3 = (bf16[128,8192]{1,0:T(8,128)(2,1)S(1)}, bf16[128,8192]{1,0:T(8,128)(2,1)}, u32[]{:S(2)}) copy-start(bf16[128,8192]{1,0:T(8,128)(2,1)} %param.9) | copy-start | bytes 6291460
  6.5 100.3 %all-gather.3.cloned.1.call-start = ((), (), s32[]{:S(2)}) async-start(), calls=%async_computation | async-start | bytes 9437184 | tf_op jit(solution)/shard_map/all_gather | solution.py:291
  7.3 194.1 %all-gather.5.cloned.1.call-start = ((), (), s32[]{:S(2)}) async-start(), calls=%async_computation.1 | async-start | bytes 9437184 | tf_op jit(solution)/shard_map/all_gather | solution.py:293
  7.3 17.2 %collective-permute-start.3 = (bf16[4,8,128,128]{3,2,1,0:T(8,128)(2,1)}, bf16[4,8,128,128]{3,2,1,0:T(8,128)(2,1)S(1)}, u32[]{:S(2)}, u32[]{:S(2)}) collective-permute-start(bf16[4,8,128,128]{3,2,1,0:T(8,128)(2,1)} %param.15), channel_id=1, source_target_pairs={{0,0},{1,64},{64,1},{65,65},{2,2},{3,66},{66,3},{67,67},{4,4},{5,6... | collective-permute-start | bytes 3145736 | tf_op jit(solution)/shard_map/ppermute | solution.py:292
  24.5 1.0 copy-start.4
  47.0 2.6 %copy-start.5 = (s32[128,64]{0,1:T(8,128)S(1)}, s32[128,64]{0,1:T(8,128)}, u32[]{:S(2)}) copy-start(s32[128,64]{0,1:T(8,128)} %param.14) | copy-start | bytes 98308
  47.0 4.2 %copy-start.7 = (s32[64,8]{0,1:T(8,128)S(1)}, s32[64,8]{0,1:T(8,128)}, u32[]{:S(2)}) copy-start(s32[64,8]{0,1:T(8,128)} %param.16) | copy-start | bytes 6148
  47.0 8.5 %copy-start.9 = (f32[2048]{0:T(1024)S(1)}, f32[2048]{0:T(1024)}, u32[]{:S(2)}) copy-start(f32[2048]{0:T(1024)} %param.17) | copy-start | bytes 24580
  47.1 10.4 %copy-start.8 = (s32[64,8]{0,1:T(8,128)S(1)}, s32[64,8]{0,1:T(8,128)}, u32[]{:S(2)}) copy-start(s32[64,8]{0,1:T(8,128)} %param.12) | copy-start | bytes 6148
  49.7 26.3 %collective-permute-start.1 = (bf16[128,4096]{1,0:T(8,128)(2,1)}, bf16[128,4096]{1,0:T(8,128)(2,1)S(1)}, u32[]{:S(2)}, u32[]{:S(2)}) collective-permute-start(bf16[128,4096]{1,0:T(8,128)(2,1)} %bitcast.19), channel_id=1, source_target_pairs={{0,1},{1,0},{2,3},{3,2},{4,5},{5,4},{6,7},{7,6},{8,9},{9,8},{10,11... | collective-permute-start | bytes 3145736 | tf_op jit(solution)/shard_map/ppermute | solution.py:301
  49.7 26.2 %collective-permute-start.2 = (bf16[128,64]{0,1:T(8,128)(2,1)S(1)}, bf16[128,64]{0,1:T(8,128)(2,1)S(1)}, u32[]{:S(2)}, u32[]{:S(2)}) collective-permute-start(bf16[128,64]{0,1:T(8,128)(2,1)S(1)} %convert_element_type.7), channel_id=1, source_target_pairs={{0,1},{1,0},{2,3},{3,2},{4,5},{5,4},{6,7},{7,6},{8,9},{9,8},{10,11... | collective-permute-start | bytes 49160 | tf_op jit(solution)/shard_map/ppermute | solution.py:315
  51.3 24.6 %collective-permute-start = (s32[64,8]{1,0:T(8,128)S(1)}, s32[64,8]{1,0:T(8,128)S(1)}, u32[]{:S(2)}, u32[]{:S(2)}) collective-permute-start(s32[64,8]{1,0:T(8,128)S(1)} %copy.20), channel_id=1, source_target_pairs={{0,0},{1,64},{64,1},{65,65},{2,2},{3,66},{66,3},{67,67},{4,4},{5,6... | collective-permute-start | bytes 6152 | tf_op jit(solution)/shard_map/ppermute | solution.py:294
  55.5 159.3 %collective-permute-start.4 = (f32[2048]{0:T(1024)S(1)}, f32[2048]{0:T(1024)S(1)}, u32[]{:S(2)}, u32[]{:S(2)}) collective-permute-start(f32[2048]{0:T(1024)S(1)} %copy-done.9), channel_id=1, source_target_pairs={{0,0},{1,64},{64,1},{65,65},{2,2},{3,66},{66,3},{67,67},{4,4},{5,6... | collective-permute-start | bytes 24584 | tf_op jit(solution)/shard_map/ppermute | solution.py:295
  120.5 2.2 copy-start.2
  214.9 2.2 copy-start.1
Sparse Core Ops, SparseCore 0:
  9.1 97.6 all-gather.2
  108.6 92.6 all-gather.4

commit v2 on v0

v2 whole, which is shorter than its diff:
```python
import functools

import jax
import jax.numpy as jnp
from jax import lax
from jax.experimental import pallas as pl
from jax.experimental.pallas import tpu as pltpu
from jax.sharding import Mesh
from jax.sharding import PartitionSpec as P

AXES = ("xh", "core", "y", "z", "xl")
DEPTH = ("z", "xl")
ROW = ("xh", "core")
BF16, F32, I32 = jnp.bfloat16, jnp.float32, jnp.int32
MESH = pl.DeviceIdType.MESH
RING = 8
CHUNKS = 4
HOPS = 14
BS = 128
ENTRIES = 8
COLUMNS = 64
ORDER = CHUNKS * RING
NOTHING = ORDER * ENTRIES


def xor(i, j):
    return lax.rem(i // 2 + j // 2, 2) * 2 + lax.rem(i + j, 2)


def greet(devices):
    barrier = pltpu.get_barrier_semaphore()
    for device in devices:
        pl.semaphore_signal(barrier, inc=1, device_id=device, device_id_type=MESH)
    pl.semaphore_wait(barrier, len(devices))


def remote(src, dst, send_sem, recv_sem, device):
    return pltpu.make_async_remote_copy(
        src_ref=src, dst_ref=dst, send_sem=send_sem, recv_sem=recv_sem, device_id=device, device_id_type=MESH
    )


class Ring:
    def __init__(self, shard, whole, z, load_sems, sems):
        self.shard, self.whole, self.z, self.load_sems, self.sems = shard, whole, z, load_sems, sems
        self.to = ({"z": lax.rem(z + 1, RING)}, {"z": lax.rem(z + RING - 1, RING)})

    def chunk(self, way, n, steps):
        behind = n // CHUNKS + steps
        slot = lax.rem(self.z + RING - behind, RING) if way == 0 else lax.rem(self.z + behind, RING)
        c = lax.rem(n, CHUNKS) if way == 0 else lax.rem(n, CHUNKS) + 2 * (n // 12)
        return slot, c

    def hop(self, way, n):
        slot, c = self.chunk(way, n, 0)
        ref = self.whole.at[slot, c]
        return remote(ref, ref, self.sems.at[0, way, n], self.sems.at[1, way, n], self.to[way])

    def start(self):
        for c in range(CHUNKS):
            self.load(c).start()
        for c in range(CHUNKS):
            self.load(c).wait()
            for way in range(2):
                self.hop(way, c).start()

    def load(self, c):
        return pltpu.make_async_copy(self.shard.at[c], self.whole.at[self.z, c], self.load_sems.at[c])

    def pump(self, way, n):
        self.hop(way, n).wait_recv()

        @pl.when(n < (10 if way == 0 else 8))
        def _():
            self.hop(way, n + 4).start()

        if way == 1:

            @pl.when(jnp.logical_and(n >= 10, n < 12))
            def _():
                self.hop(way, n + 2).start()

    def pumps(self, first, last):
        @pl.loop(first, last)
        def _(n):
            for way in range(2):
                self.pump(way, n)

    def end(self):
        @pl.loop(0, HOPS)
        def _(n):
            for way in range(2):
                self.hop(way, n).wait_send()


def write_tables(columns_ref, base, z, parity, table_ref):
    columns = columns_ref[...] - base
    columns = jnp.concatenate([columns, columns], axis=1)
    lane = lax.broadcasted_iota(I32, columns.shape, 1)
    entry = lax.broadcasted_iota(I32, columns.shape, 0)
    last = jnp.full(columns.shape, NOTHING, I32)
    before = jnp.zeros(columns.shape, I32)
    for t in range(ORDER):
        if t < CHUNKS:
            slot, c = z, t
        else:
            n, way = (t - CHUNKS) // 2, (t - CHUNKS) % 2
            steps = n // CHUNKS + 1
            slot = lax.rem(z + (RING - steps if way == 0 else steps), RING)
            c = n % CHUNKS + (2 if way == 1 and n >= 12 else 0)
        row = slot * 8 + parity * CHUNKS + c
        column = jnp.sum(jnp.where(lane == row, columns, 0), axis=1, keepdims=True)
        hit = lane == column
        place = jnp.sum(jnp.where(hit, last, 0), axis=1, keepdims=True)
        before = jnp.where(lane == t, place, before)
        newest = jnp.max(jnp.where(hit, t * ENTRIES + entry, -1), axis=0, keepdims=True)
        last = jnp.where(newest >= 0, newest, last)
    table_ref[pl.ds(0, 8), :] = before
    table_ref[pl.ds(8, 8), :] = last


def use(x_ref, ring, sums, table, slot, c, t):
    lhs = x_ref[slot * CHUNKS + c]
    for k in range(0, ENTRIES, 2):
        rhs = jnp.concatenate([ring.whole[slot, c, k], ring.whole[slot, c, k + 1]], axis=1)
        out = jnp.dot(lhs, rhs, preferred_element_type=F32)
        sums[t * ENTRIES + k] = sums[table[k, t]] + out[:, :BS]
        sums[t * ENTRIES + k + 1] = sums[table[k + 1, t]] + out[:, BS:]


def use_all(x_ref, ring, sums, table, pumped):
    @pl.loop(0, CHUNKS)
    def _(c):
        use(x_ref, ring, sums, table, ring.z, c, c)

    def arrived(n, way):
        slot, c = ring.chunk(way, n, 1)
        use(x_ref, ring, sums, table, slot, c, CHUNKS + 2 * n + way)

    @pl.loop(0, pumped)
    def _(n):
        for way in range(2):
            arrived(n, way)

    @pl.loop(pumped, HOPS)
    def _(n):
        for way in range(2):
            ring.pump(way, n)
        for way in range(2):
            arrived(n, way)


FIRST = ((2, 1), (2, 3))
LANDS = ((3, 0), (1, 0))


def reduce_scatter(other, near, half, source, mine, got, out1, in1, out2, in2, sems, finish, between):
    exchanged = {}
    order = [(2, 0), (2, 1), (1, 0), (3, 1), (3, 0), (1, 1), (0, 0), (0, 1)]
    for n, (g, h) in enumerate(order):
        exchanged[g, h] = remote(
            source(g, h), got.at[g, pl.ds(h * half, half)], sems.at[0, n], sems.at[1, n], other
        )
        exchanged[g, h].start()
    between(0)

    def both(g, h, c):
        return mine(g, h, c) + got[g, h * half + c].astype(F32)

    firsts = {}
    for s in range(2):
        for h in range(2):
            g = FIRST[h][s]
            exchanged[g, h].wait_recv()

            @pl.loop(0, half)
            def _(c):
                out1[h, s, c] = both(g, h, c).astype(BF16)

            n = 8 + 2 * h + s
            firsts[h, s] = remote(out1.at[h, s], in1.at[h, s], sems.at[0, n], sems.at[1, n], near[h])
            firsts[h, s].start()
    between(1)
    seconds = {}
    for h in range(2):
        g = LANDS[h][0]
        exchanged[g, h].wait_recv()
        firsts[h, 0].wait_recv()

        @pl.loop(0, half)
        def _(c):
            out2[h, c] = (both(g, h, c) + in1[h, 0, c].astype(F32)).astype(BF16)

        seconds[h] = remote(out2.at[h], in2.at[h], sems.at[0, 12 + h], sems.at[1, 12 + h], near[1 - h])
        seconds[h].start()
    between(2)
    for h in range(2):
        exchanged[0, h].wait_recv()
        firsts[h, 1].wait_recv()
        seconds[h].wait_recv()
        finish(h, lambda c: both(0, h, c) + in1[h, 1, c].astype(F32) + in2[h, c].astype(F32))
    for copy in [*exchanged.values(), *firsts.values(), *seconds.values()]:
        copy.wait_send()


def first_kernel(
    w1, w2, acts, act_mask, mask2, columns1, columns2, bias2,
    keep, send, w2_out, mask2_out, columns2_out, bias2_out,
    whole, sums, x0, mine, taken, mask_taken, table_v, table,
    load_sems, ring_sems, mine_sems, taken_sems, small_sems, swap_sems, table_sem,
):
    xh, core, y, z, xl = (lax.axis_index(a) for a in AXES)
    x = xh * 2 + xl
    beside = {"xl": 1 - xl}
    home = {"core": 1 - core, "xl": 1 - xl}
    away = xl != core
    ring = Ring(w1, whole, z, load_sems, ring_sems)
    greet((*ring.to, beside, home))
    ring.start()

    def part(s, parity):
        return acts.at[:, pl.ds((s * 8 + parity * CHUNKS) * BS, CHUNKS * BS)]

    def place(ref, s):
        return ref.at[:, pl.ds(s * CHUNKS * BS, CHUNKS * BS)]

    small = [
        remote(act_mask, mask_taken, small_sems.at[0, 0], small_sems.at[1, 0], beside),
        remote(mask2, mask2_out.at[xl], small_sems.at[0, 1], small_sems.at[1, 1], beside),
    ]
    for copy in small:
        copy.start()
    given = [
        remote(part(s, 1 - xl), place(taken, s), taken_sems.at[0, s], taken_sems.at[1, s], beside)
        for s in range(RING)
    ]
    own = [pltpu.make_async_copy(part(s, xl), place(mine, s), mine_sems.at[s]) for s in range(RING)]
    for copy in (*given, *own):
        copy.start()
    moves = ((w2, w2_out), (columns2, columns2_out), (bias2, bias2_out))

    @pl.when(away)
    def _():
        for n, (src, dst) in enumerate(moves):
            remote(src, dst, swap_sems.at[0, n], swap_sems.at[1, n], home).start()

    @pl.when(jnp.logical_not(away))
    def _():
        pltpu.make_async_copy(w2, w2_out, swap_sems.at[0, 0]).start()
        columns2_out[...] = columns2[...]
        bias2_out[...] = bias2[...]

    mask2_out[xl] = mask2[...]
    write_tables(columns1, y * COLUMNS, z, xl, table_v)
    sums[NOTHING] = jnp.zeros(sums.shape[1:], F32)

    def masked(blocks, mask_ref, first_row):
        live = mask_ref[...].astype(F32)
        for i in range(ORDER):
            b = i // CHUNKS * 8 + i % CHUNKS
            column = jnp.where(xl == 0, live[:, b : b + 1], live[:, b + CHUNKS : b + CHUNKS + 1])
            factor = jnp.broadcast_to(column, (live.shape[0], BS)).astype(BF16)
            x0[i, pl.ds(pl.multiple_of(first_row, BS), BS), :] = blocks[:, i * BS : (i + 1) * BS] * factor

    for copy in own:
        copy.wait()
    masked(mine, act_mask, xl * BS)
    to_scalars = pltpu.make_async_copy(table_v, table, table_sem)
    to_scalars.start()
    ring.pumps(0, 3)
    for copy in (*small, *given):
        copy.wait_recv()
    masked(taken, mask_taken, (1 - xl) * BS)
    to_scalars.wait()
    use_all(x0, ring, sums, table, 3)

    for half, ref in enumerate((keep, send)):

        @pl.loop(0, COLUMNS // 2)
        def _(p):
            chip = xor(p // 8, x)
            parity = lax.rem(core + half, 2)
            j = (chip * 2 + lax.rem(p // 4, 2)) * 8 + parity * 4 + lax.rem(p, 4)
            ref[p] = sums[table[8, j]]

    for copy in (*small, *given):
        copy.wait_send()

    @pl.when(away)
    def _():
        for n, (src, dst) in enumerate(moves):
            remote(src, dst, swap_sems.at[0, n], swap_sems.at[1, n], home).wait()

    @pl.when(jnp.logical_not(away))
    def _():
        pltpu.make_async_copy(w2, w2_out, swap_sems.at[0, 0]).wait()

    ring.end()


def second_kernel(
    w2, keep, send, mask2, bias1, columns2, bias2, out,
    whole, sums, hid, live, table_v, table, fin, sent,
    got1, out1a, in1a, out2a, in2a, got2, out1b, in1b, out2b, in2b,
    load_sems, ring_sems, keep_sem, table_sem, sems1, sems2, spread_sems, back_sems,
):
    xh, core, y, z, xl = (lax.axis_index(a) for a in AXES)
    x = xh * 2 + xl
    flip_y = y + 1 - 2 * lax.rem(y, 2)
    other = {"core": 1 - core}
    home = {"core": 1 - core, "xl": 1 - xl}
    away = xl != core
    near_x = ({"xl": 1 - xl}, {"xh": 1 - xh, "xl": 1 - xl})
    chips = (xh * 2 + 1 - xl, 3 - x)
    near_y = ({"y": flip_y}, {"y": 3 - y})
    ring = Ring(w2, whole, z, load_sems, ring_sems)
    greet((*ring.to, other, home, *near_x, *near_y))
    fetch = pltpu.make_async_copy(keep, sums.at[pl.ds(0, COLUMNS // 2)], keep_sem)
    fetch.start()
    ring.start()

    half = 4

    def piece(chip, h):
        return hid.at[pl.ds(chip * 8 + h * half, half)]

    copies = []

    def spread(chip, h, to, n):
        ref = piece(chip, h)
        copy = remote(ref, ref, spread_sems.at[0, n], spread_sems.at[1, n], near_x[to])
        copy.start()
        copies.append(copy)
        return copy

    given = {}

    def finish_hidden(h, total):
        for c in range(half):
            n = h * half + c
            j = (x * 2 + h) * 8 + core * 4 + c
            hid[x * 8 + n] = (jnp.maximum(total(c) + bias1[pl.ds(j, 1), :], 0.0) * live[n].astype(F32)).astype(BF16)
        for to in (1 - h, h):
            given[h, to] = spread(x, h, to, 2 * h + to)

    def between_hidden(stage):
        if stage == 0:
            mask = mask2[...].astype(F32)
            lane = lax.broadcasted_iota(I32, mask.shape[1:], 1)
            for n in range(8):
                j = (x * 2 + n // 4) * 8 + core * 4 + n % 4
                for s in range(2):
                    column = jnp.sum(jnp.where(lane == j, mask[s], 0.0), axis=1, keepdims=True)
                    live[n, s * BS : (s + 1) * BS, :] = jnp.broadcast_to(column, (BS, BS)).astype(BF16)
            fetch.wait()
        elif stage == 1:
            write_tables(columns2, x * COLUMNS, z, core, table_v)
            ring.pumps(0, 1)
        else:
            ring.pumps(1, 3)

    reduce_scatter(
        other, near_x, half,
        lambda g, h: send.at[pl.ds(g * 8 + h * half, half)],
        lambda g, h, c: sums[g * 8 + h * half + c],
        got1, out1a, in1a, out2a, in2a, sems1, finish_hidden, between_hidden,
    )
    to_scalars = pltpu.make_async_copy(table_v, table, table_sem)
    to_scalars.start()
    ring.pumps(3, 5)
    for h in range(2):
        given[h, 1 - h].wait_recv()
        spread(chips[1 - h], h, h, 4 + h)
    ring.pumps(5, 6)
    for h in range(2):
        given[h, h].wait_recv()
    for copy in copies[4:]:
        copy.wait_recv()
    to_scalars.wait()
    sums[NOTHING] = jnp.zeros(sums.shape[1:], F32)
    ring.pumps(6, 8)
    use_all(hid, ring, sums, table, 8)

    half = 8

    def column(g, n):
        return xor(y, g) * 16 + n

    def rows_of(c):
        return pl.ds(pl.multiple_of(c * BS, BS), BS)

    def source(g, h):
        @pl.loop(0, half)
        def _(c):
            n = h * half + c
            sent[g, n] = sums[table[8, column(g, n)], rows_of(1 - core), :].astype(BF16)

        return sent.at[g, pl.ds(h * half, half)]

    def back(h):
        ref = pl.ds(h * half * BS, half * BS)
        return remote(fin.at[:, ref], out.at[:, ref], back_sems.at[0, h], back_sems.at[1, h], home)

    def finish_result(h, total):
        for c in range(half):
            n = h * half + c
            value = jnp.maximum(total(c) + bias2[pl.ds(n, 1), :], 0.0)
            fin[:, n * BS : (n + 1) * BS] = value.astype(BF16)

        @pl.when(away)
        def _():
            back(h).start()

    reduce_scatter(
        other, near_y, half, source,
        lambda g, h, c: sums[table[8, column(g, h * half + c)], rows_of(core), :],
        got2, out1b, in1b, out2b, in2b, sems2, finish_result, lambda stage: None,
    )

    @pl.when(away)
    def _():
        for h in range(2):
            back(h).wait()

    @pl.when(jnp.logical_not(away))
    def _():
        out[...] = fin[...]

    for copy in copies:
        copy.wait_send()
    ring.end()


ANY = pl.BlockSpec(memory_space=pl.ANY)
VMEM = pl.BlockSpec(memory_space=pltpu.VMEM)


def ring_scratch(rows):
    return (
        pltpu.VMEM((RING, CHUNKS, ENTRIES, BS, BS), BF16),
        pltpu.VMEM((NOTHING + 1, rows, BS), F32),
    )


RING_SEMS = (pltpu.SemaphoreType.DMA((CHUNKS,)), pltpu.SemaphoreType.DMA((2, 2, HOPS)))
TABLES = (pltpu.VMEM((16, 128), I32), pltpu.SMEM((16, 128), I32))


def halving_scratch(blocks, rows, exchanged):
    half = (blocks // 2, rows, BS)
    return (
        pltpu.VMEM((4, blocks, rows, BS), exchanged),
        pltpu.VMEM((2, 2, *half), BF16),
        pltpu.VMEM((2, 2, *half), BF16),
        pltpu.VMEM((2, *half), BF16),
        pltpu.VMEM((2, *half), BF16),
    )


def params(collective_id):
    return pltpu.CompilerParams(collective_id=collective_id, has_side_effects=True, vmem_limit_bytes=67_000_000)


def on_device(acts, act_mask, w1, cols1, bias1, mask2, w2, cols2, bias2):
    n = acts.shape[0]
    dma = pltpu.SemaphoreType.DMA
    shape = jax.ShapeDtypeStruct
    keep, send, w2, mask2, columns2, bias2 = pl.pallas_call(
        first_kernel,
        out_shape=(
            shape((COLUMNS // 2, 2 * n, BS), F32),
            shape((COLUMNS // 2, 2 * n, BS), F32),
            shape(w2.shape, BF16),
            shape((2, *mask2.shape), I32),
            shape((ENTRIES, 64), I32),
            shape((16, BS), F32),
        ),
        in_specs=[ANY, ANY, ANY, VMEM, VMEM, VMEM, VMEM, VMEM],
        out_specs=(VMEM,) * 6,
        scratch_shapes=[
            *ring_scratch(2 * n),
            pltpu.VMEM((ORDER, 2 * n, BS), BF16),
            pltpu.VMEM((n, ORDER * BS), BF16),
            pltpu.VMEM((n, ORDER * BS), BF16),
            pltpu.VMEM(act_mask.shape, I32),
            *TABLES,
            *RING_SEMS,
            dma((RING,)),
            dma((2, RING)),
            dma((2, 2)),
            dma((2, 3)),
            dma(()),
        ],
        compiler_params=params(0),
        name="first",
    )(w1, w2, acts, act_mask, mask2, cols1.T, cols2.T, bias2.reshape(16, BS))
    return pl.pallas_call(
        second_kernel,
        out_shape=shape((n, 16 * BS), BF16),
        in_specs=[ANY, ANY, ANY, VMEM, VMEM, VMEM, VMEM],
        out_specs=VMEM,
        scratch_shapes=[
            *ring_scratch(2 * n),
            pltpu.VMEM((ORDER, 2 * n, BS), BF16),
            pltpu.VMEM((8, 2 * n, BS), BF16),
            *TABLES,
            pltpu.VMEM((n, 16 * BS), BF16),
            pltpu.VMEM((4, 16, n, BS), BF16),
            *halving_scratch(8, 2 * n, F32),
            *halving_scratch(16, n, BF16),
            *RING_SEMS,
            dma(()),
            dma(()),
            dma((2, 14)),
            dma((2, 14)),
            dma((2, 6)),
            dma((2, 2)),
        ],
        compiler_params=params(1),
        name="second",
    )(w2, keep, send, mask2, bias1.reshape(COLUMNS, BS), columns2, bias2)


def solution(mesh):
    finer = Mesh(mesh.devices.reshape(2, 2, mesh.shape["col"], RING, 2), AXES)
    in_specs = (
        P(DEPTH, ROW),
        P(DEPTH, ROW),
        P((*ROW, *DEPTH), "y", None, None),
        P(ROW, "y"),
        P("y"),
        P(DEPTH, "y"),
        P(("y", *DEPTH), ROW, None, None),
        P("y", ROW),
        P((*ROW, "y")),
    )
    out_specs = P(DEPTH, (*ROW, "y"))
    return jax.shard_map(on_device, mesh=finer, in_specs=in_specs, out_specs=out_specs, check_vma=False)
```

time: 907 us -> 220 us (0.24); the launches traced: 896 us -> 219 us
  waiting for transfers between devices: 433 us -> 0 us
  Pallas kernels: 0 us -> 215 us
  other arithmetic: 208 us -> 0 us
  matrix products: 99.2 us -> 0 us
  local copies, waits for them, and re-layouts: 76.5 us -> 4.84 us
  blocking collectives: 54.2 us -> 0 us
  between operations: 13.2 us -> 0.02 us
  starting transfers between devices: 11.1 us -> 0 us
    all_gather x3 -> x0, waiting for transfers between devices: 290 us -> none  [the longest x2 214 us: whole_of(): result = lax.all_gather(result, axes[number], axis=dim, tiled=True)]
    pallas_call x0 -> x2, Pallas kernels: none -> 215 us  [the longest x1 117 us: on_device(): pl.pallas_call(second_kernel, out_shape=shape((n, 16 * BS), BF16), in_spe...]
    scatter-add x32 -> x0, other arithmetic: 199 us -> none  [advance(): return total.at[:, wanted.reshape(-1)].add(flat_product)]
    all_to_all x2 -> x0, waiting for transfers between devices: 142 us -> none  [the longest x1 141 us: summed_on_arrival(): parts = lax.all_to_all(split_up(x, dim, count), axis, 0, 0, tiled=True)]
    dot_general x32 -> x0, matrix products: 99.2 us -> none  [advance(): jnp.einsum('tws,wish->twih', incoming_rows, block_list, preferred_element...]
    reshape x64 -> x0, local copies, waits for them, and re-layouts: 64.1 us -> none  [the longest x32 61.5 us: advance(): flat_product = product.reshape(product.shape[0], -1, product.shape[-1])]
    all_to_all x1 -> x0, blocking collectives: 54.2 us -> none  [summed_on_arrival(): parts = lax.all_to_all(split_up(x, dim, count), axis, 0, 0, tiled=True)]
    all_to_all x2 -> x0, starting transfers between devices: 11.1 us -> none  [the longest x1 5.66 us: summed_on_arrival(): parts = lax.all_to_all(split_up(x, dim, count), axis, 0, 0, tiled=True)]
  transfers between devices with their start and end apart: 5 -> 0, of which waited for: 5 -> 0; matrix products, arithmetic and copies ran while one was open for 22% -> 0% of each run, Pallas kernels for 0% -> 0%
where the time goes in v2:
time: 220 us; the launch traced here: 219 us
  Pallas kernels  215 us (98%)
  local copies, waits for them, and re-layouts  4.84 us (2%)
    pallas_call x1, Pallas kernels, on_device(): pl.pallas_call(second_kernel, out_shape=shape((n, 16 * BS), BF16), in_spe...  117 us
    pallas_call x1, Pallas kernels, on_device(): pl.pallas_call(first_kernel, out_shape=(shape((COLUMNS // 2, 2 * n, BS),...  97.1 us
    unnamed x3, local copies, waits for them, and re-layouts  4.84 us

profile of v2, /device:TPU:1, one launch (start us, length us, event | category | flops | bytes accessed | tf_op | source)
XLA Modules:
  0.0 219.5 jit_solution(13307736872899019550)
XLA Ops:
  0.0 1.5 copy.10.act_mask
  1.5 1.5 copy.11.mask2
  3.0 97.1 %first.1 = (f32[32,256,128]{2,1,0:T(8,128)}, f32[32,256,128]{2,1,0:T(8,128)}, bf16[4,8,128,128]{3,2,1,0:T(8,128)(2,1)}, s32[2,128,64]{2,1,0:T(8,128)}, s32[8,64]{1,0:T(8,128)}, /*index=5*/f32[16,128]{1,0:T(8,128)}) custom-call(bf16[4,8,128,128]{3,2,1,0:T(8,128)(2,1)} %w1.1, bf16[4,8,128,128]{3,2,1,0:T(8,128)(2,1)} %w2.1, bf16[128,8192]{1,0:T(8,128)(2,1)} %acts.1, ...), custom_call_target="tpu_custom_call" | custom-call | tf_op jit(solution)/shard_map/first/pallas_call | solution.py:468
  100.1 117.5 %second.1 = bf16[128,2048]{1,0:T(8,128)(2,1)} custom-call(bf16[4,8,128,128]{3,2,1,0:T(8,128)(2,1)} %get-tuple-element.11.w2, f32[32,256,128]{2,1,0:T(8,128)} %get-tuple-element.12.keep, f32[32,256,128]{2,1,0:T(8,128)} %get-tuple-element.13.send, s32[2,128,64]{2,1,0:T(8,128)} %get-tuple-element.14.mask2, f32[64,128]{1,0:T(8,128)} %bitcast.4, ...), custom_call_target="tpu_custom_call" | custom-call | tf_op jit(solution)/shard_map/second/pallas_call | solution.py:497
  217.6 1.9 copy.13

commit v3 on v0

v3 whole, which is shorter than its diff:
```python
import jax
import jax.numpy as jnp
from jax import lax
from jax.experimental import pallas as pl
from jax.experimental.pallas import tpu as pltpu
from jax.sharding import Mesh
from jax.sharding import PartitionSpec as P

AXES = ("xh", "core", "y", "z", "xl")
DEPTH = ("z", "xl")
ROW = ("xh", "core")
BF16, F32, I32 = jnp.bfloat16, jnp.float32, jnp.int32
MESH = pl.DeviceIdType.MESH
RING = 8
CHUNKS = 4
HOPS = 14
BS = 128
ENTRIES = 8
COLUMNS = 64
ORDER = CHUNKS * RING
NOTHING = ORDER * ENTRIES


def xor(i, j):
    return lax.rem(i // 2 + j // 2, 2) * 2 + lax.rem(i + j, 2)


def greet(devices):
    barrier = pltpu.get_barrier_semaphore()
    for device in devices:
        pl.semaphore_signal(barrier, inc=1, device_id=device, device_id_type=MESH)
    pl.semaphore_wait(barrier, len(devices))


def remote(src, dst, send_sem, recv_sem, device):
    return pltpu.make_async_remote_copy(
        src_ref=src, dst_ref=dst, send_sem=send_sem, recv_sem=recv_sem, device_id=device, device_id_type=MESH
    )


class Ring:
    def __init__(self, shard, whole, z, load_sems, sems):
        self.shard, self.whole, self.z, self.load_sems, self.sems = shard, whole, z, load_sems, sems
        self.to = ({"z": lax.rem(z + 1, RING)}, {"z": lax.rem(z + RING - 1, RING)})

    def chunk(self, way, n, steps):
        behind = n // CHUNKS + steps
        slot = lax.rem(self.z + RING - behind, RING) if way == 0 else lax.rem(self.z + behind, RING)
        c = lax.rem(n, CHUNKS) if way == 0 else lax.rem(n, CHUNKS) + 2 * (n // 12)
        return slot, c

    def hop(self, way, n):
        slot, c = self.chunk(way, n, 0)
        ref = self.whole.at[slot, c]
        return remote(ref, ref, self.sems.at[0, way, n], self.sems.at[1, way, n], self.to[way])

    def start(self):
        for c in range(CHUNKS):
            self.load(c).start()
        for c in range(CHUNKS):
            self.load(c).wait()
            for way in range(2):
                self.hop(way, c).start()

    def send_own(self):
        for c in range(CHUNKS):
            for way in range(2):
                self.hop(way, c).start()

    def load(self, c):
        return pltpu.make_async_copy(self.shard.at[c], self.whole.at[self.z, c], self.load_sems.at[c])

    def pump(self, way, n):
        self.hop(way, n).wait_recv()

        @pl.when(n < (10 if way == 0 else 8))
        def _():
            self.hop(way, n + 4).start()

        if way == 1:

            @pl.when(jnp.logical_and(n >= 10, n < 12))
            def _():
                self.hop(way, n + 2).start()

    def pumps(self, first, last):
        @pl.loop(first, last)
        def _(n):
            for way in range(2):
                self.pump(way, n)

    def end(self):
        @pl.loop(0, HOPS)
        def _(n):
            for way in range(2):
                self.hop(way, n).wait_send()


def write_tables(columns_ref, base, z, parity, table_ref):
    columns = columns_ref[...] - base
    columns = jnp.concatenate([columns, columns], axis=1)
    lane = lax.broadcasted_iota(I32, columns.shape, 1)
    entry = lax.broadcasted_iota(I32, columns.shape, 0)
    last = jnp.full(columns.shape, NOTHING, I32)
    before = jnp.zeros(columns.shape, I32)
    for t in range(ORDER):
        if t < CHUNKS:
            slot, c = z, t
        else:
            n, way = (t - CHUNKS) // 2, (t - CHUNKS) % 2
            steps = n // CHUNKS + 1
            slot = lax.rem(z + (RING - steps if way == 0 else steps), RING)
            c = n % CHUNKS + (2 if way == 1 and n >= 12 else 0)
        row = slot * 8 + parity * CHUNKS + c
        column = jnp.sum(jnp.where(lane == row, columns, 0), axis=1, keepdims=True)
        hit = lane == column
        place = jnp.sum(jnp.where(hit, last, 0), axis=1, keepdims=True)
        before = jnp.where(lane == t, place, before)
        newest = jnp.max(jnp.where(hit, t * ENTRIES + entry, -1), axis=0, keepdims=True)
        last = jnp.where(newest >= 0, newest, last)
    table_ref[pl.ds(0, 8), :] = before
    table_ref[pl.ds(8, 8), :] = last


def use(x_ref, ring, sums, table, slot, c, t):
    lhs = x_ref[slot * CHUNKS + c]
    for k in range(0, ENTRIES, 2):
        rhs = jnp.concatenate([ring.whole[slot, c, k], ring.whole[slot, c, k + 1]], axis=1)
        out = jnp.dot(lhs, rhs, preferred_element_type=F32)
        sums[t * ENTRIES + k] = sums[table[k, t]] + out[:, :BS]
        sums[t * ENTRIES + k + 1] = sums[table[k + 1, t]] + out[:, BS:]


def use_own(x_ref, ring, sums, table):
    @pl.loop(0, CHUNKS)
    def _(c):
        use(x_ref, ring, sums, table, ring.z, c, c)


def use_arrived(x_ref, ring, sums, table, first, last, pumped):
    @pl.loop(first, last)
    def _(n):
        if not pumped:
            for way in range(2):
                ring.pump(way, n)
        for way in range(2):
            slot, c = ring.chunk(way, n, 1)
            use(x_ref, ring, sums, table, slot, c, CHUNKS + 2 * n + way)


FIRST = ((2, 1), (2, 3))
LANDS = ((3, 0), (1, 0))
UNITS = 16
PART = 4


def reduce_scatter(other, near, mine, theirs, sent, got, out1, in1, out2, in2, sems, finish, between):
    def start(n, src, dst, device):
        copy = remote(src, dst, sems.at[0, n], sems.at[1, n], device)
        copy.start()
        return copy

    def unit(h, s, c):
        return (2 * h + s) * PART + c

    exchanged, firsts, seconds = {}, {}, {}
    order = [(2, 0), (2, 1), (1, 0), (3, 1), (3, 0), (1, 1), (0, 0), (0, 1)]
    for s in range(2):
        for g, h in order:

            @pl.loop(0, PART)
            def _(c):
                n = unit(h, s, c)
                sent[g, n] = theirs(g, n).astype(BF16)

            ref = pl.ds(unit(h, s, 0), PART)
            exchanged[g, h, s] = start(len(exchanged), sent.at[g, ref], got.at[g, ref], other)
    between(0)

    def both(g, h, s, c):
        n = unit(h, s, c)
        return mine(g, n) + got[g, n].astype(F32)

    def first(s, step):
        for h in range(2):
            g = FIRST[h][step]
            exchanged[g, h, s].wait_recv()

            @pl.loop(0, PART)
            def _(c):
                out1[h, step, s, c] = both(g, h, s, c).astype(BF16)

            n = 16 + 4 * s + 2 * step + h
            firsts[h, s, step] = start(n, out1.at[h, step, s], in1.at[h, step, s], near[h])

    def second(s):
        for h in range(2):
            g = LANDS[h][0]
            exchanged[g, h, s].wait_recv()
            firsts[h, s, 0].wait_recv()

            @pl.loop(0, PART)
            def _(c):
                out2[h, s, c] = (both(g, h, s, c) + in1[h, 0, s, c].astype(F32)).astype(BF16)

            seconds[h, s] = start(24 + 2 * s + h, out2.at[h, s], in2.at[h, s], near[1 - h])

    first(0, 0)
    first(0, 1)
    first(1, 0)
    between(1)
    second(0)
    first(1, 1)
    second(1)
    between(2)
    for s in range(2):
        for h in range(2):
            exchanged[0, h, s].wait_recv()
            firsts[h, s, 1].wait_recv()
            seconds[h, s].wait_recv()
            finish(
                h, s, lambda c: both(0, h, s, c) + in1[h, 1, s, c].astype(F32) + in2[h, s, c].astype(F32)
            )
    for copy in [*exchanged.values(), *firsts.values(), *seconds.values()]:
        copy.wait_send()


def kernel(
    w1, w2, acts, act_mask, mask2, columns1, columns2, bias1, bias2, out,
    whole1, whole2, sums, x0, live, mask_taken, masks2, columns_in, bias_in, table_v1, table_v2, table1, table2,
    sent, out1, out2, got_a, in1_a, in2_a, got_b, in1_b, in2_b, fin,
    load_sems, ring1_sems, ring2_sems, mine_sems, taken_sems, small_sems, swap_sems, table_sems,
    sems_a, sems_b, spread_sems, back_sems,
):
    xh, core, y, z, xl = (lax.axis_index(a) for a in AXES)
    x = xh * 2 + xl
    other = {"core": 1 - core}
    home = {"core": 1 - core, "xl": 1 - xl}
    away = xl != core
    near_x = ({"xl": 1 - xl}, {"xh": 1 - xh, "xl": 1 - xl})
    chips = (xh * 2 + 1 - xl, 3 - x)
    near_y = ({"y": y + 1 - 2 * lax.rem(y, 2)}, {"y": 3 - y})
    beside = near_x[0]
    ring1 = Ring(w1, whole1, z, load_sems, ring1_sems)
    ring2 = Ring(w2, whole2, z, load_sems, ring2_sems)
    greet((*ring1.to, other, home, *near_x, *near_y))

    def rows_of(c):
        return pl.ds(pl.multiple_of(c * BS, BS), BS)

    ring1.start()
    small = [
        remote(act_mask, mask_taken, small_sems.at[0, 0], small_sems.at[1, 0], beside),
        remote(mask2, masks2.at[xl], small_sems.at[0, 1], small_sems.at[1, 1], beside),
    ]
    for copy in small:
        copy.start()

    def block(i, parity):
        b = i // CHUNKS * 8 + parity * CHUNKS + lax.rem(i, CHUNKS)
        return acts.at[:, pl.ds(pl.multiple_of(b * BS, BS), BS)]

    def given(i):
        return remote(block(i, 1 - xl), x0.at[i, rows_of(xl)], taken_sems.at[0, i], taken_sems.at[1, i], beside)

    def own(i):
        return pltpu.make_async_copy(block(i, xl), x0.at[i, rows_of(xl)], mine_sems.at[i])

    @pl.loop(0, ORDER)
    def _(i):
        given(i).start()
        own(i).start()

    moves = ((columns2, columns_in), (bias2, bias_in), (w2, whole2.at[z]))

    def swaps():
        return [remote(src, dst, swap_sems.at[0, n], swap_sems.at[1, n], home) for n, (src, dst) in enumerate(moves)]

    def stay():
        return pltpu.make_async_copy(w2, whole2.at[z], swap_sems.at[0, 2])

    @pl.when(away)
    def _():
        for copy in swaps():
            copy.start()

    @pl.when(jnp.logical_not(away))
    def _():
        stay().start()
        columns_in[...] = columns2[...]
        bias_in[...] = bias2[...]

    masks2[xl] = mask2[...]
    write_tables(columns1, y * COLUMNS, z, xl, table_v1)
    sums[NOTHING] = jnp.zeros(sums.shape[1:], F32)

    def by_rows(mask):
        mask = mask.astype(F32)
        return jnp.concatenate([mask, mask], axis=0).T

    def masked(mask_ref, rows):
        factors = by_rows(mask_ref[...])
        for i in range(ORDER):
            b = i // CHUNKS * 8 + i % CHUNKS
            column = jnp.where(xl == 0, factors[:, b : b + 1], factors[:, b + CHUNKS : b + CHUNKS + 1])
            factor = jnp.broadcast_to(column, (BS, BS)).astype(BF16)
            x0[i, rows, :] = x0[i, rows, :] * factor

    @pl.loop(0, ORDER)
    def _(i):
        own(i).wait()

    masked(act_mask, rows_of(xl))
    to_scalars1 = pltpu.make_async_copy(table_v1, table1, table_sems.at[0])
    to_scalars1.start()
    ring1.pumps(0, 3)
    for copy in small:
        copy.wait_recv()

    @pl.loop(0, ORDER)
    def _(i):
        given(i).wait_recv()

    masked(mask_taken, rows_of(1 - xl))
    to_scalars1.wait()

    use_own(x0, ring1, sums, table1)
    use_arrived(x0, ring1, sums, table1, 0, 3, True)
    use_arrived(x0, ring1, sums, table1, 3, 5, False)
    for s in range(2):
        rows = by_rows(masks2[s])
        lane = lax.broadcasted_iota(I32, rows.shape, 1)
        for n in range(8):
            j = (x * 2 + n // 4) * 8 + core * 4 + n % 4
            column = jnp.sum(jnp.where(lane == j, rows, 0.0), axis=1, keepdims=True)
            live[2 * n + s] = jnp.broadcast_to(column, (BS, BS)).astype(BF16)

    @pl.when(away)
    def _():
        for copy in swaps():
            copy.wait_recv()

    @pl.when(jnp.logical_not(away))
    def _():
        stay().wait()

    write_tables(columns_in, x * COLUMNS, z, core, table_v2)
    use_arrived(x0, ring1, sums, table1, 5, 12, False)
    ring2.send_own()
    to_scalars2 = pltpu.make_async_copy(table_v2, table2, table_sems.at[1])
    to_scalars2.start()
    use_arrived(x0, ring1, sums, table1, 12, HOPS, False)

    def hidden_sum(parity):
        def unit(g, n):
            j = (xor(g, x) * 2 + n // 8) * 8 + parity * 4 + lax.rem(n // 2, 4)
            return sums[table1[8, j], rows_of(lax.rem(n, 2)), :]

        return unit

    def piece(chip, h, s):
        return x0.at[pl.ds(chip * 8 + h * 4 + s * 2, 2)]

    copies, spreads = [], {}

    def spread(chip, h, s, to):
        ref, n = piece(chip, h, s), len(copies)
        copy = remote(ref, ref, spread_sems.at[0, n], spread_sems.at[1, n], near_x[to])
        copy.start()
        copies.append(copy)
        return copy

    def finish_hidden(h, s, total):
        for c in range(PART):
            n = (2 * h + s) * PART + c
            j = (x * 2 + n // 8) * 8 + core * 4 + n // 2 % 4
            value = jnp.maximum(total(c) + bias1[pl.ds(j, 1), :], 0.0) * live[n].astype(F32)
            x0[x * 8 + n // 2, pl.ds(n % 2 * BS, BS), :] = value.astype(BF16)
        for to in (1 - h, h):
            spreads[h, s, to] = spread(x, h, s, to)

    def between_hidden(stage):
        if stage > 0:
            ring2.pumps(stage - 1, stage)

    reduce_scatter(
        other, near_x, hidden_sum(core), hidden_sum(1 - core), sent, got_a, out1, in1_a, out2, in2_a, sems_a,
        finish_hidden, between_hidden,
    )
    ring2.pumps(2, 4)
    last = []
    for s in range(2):
        for h in range(2):
            spreads[h, s, 1 - h].wait_recv()
            last.append(spread(chips[1 - h], h, s, h))
    ring2.pumps(4, 6)
    for s in range(2):
        for h in range(2):
            spreads[h, s, h].wait_recv()
    for copy in last:
        copy.wait_recv()
    to_scalars2.wait()

    use_own(x0, ring2, sums, table2)
    use_arrived(x0, ring2, sums, table2, 0, 6, True)
    use_arrived(x0, ring2, sums, table2, 6, HOPS, False)

    def result_sum(half):
        def unit(g, n):
            return sums[table2[8, xor(g, y) * UNITS + n], rows_of(half), :]

        return unit

    def back(h, s):
        ref, n = pl.ds((2 * h + s) * PART * BS, PART * BS), 2 * h + s
        return remote(fin.at[:, ref], out.at[:, ref], back_sems.at[0, n], back_sems.at[1, n], home)

    def finish_result(h, s, total):
        for c in range(PART):
            n = (2 * h + s) * PART + c
            value = jnp.maximum(total(c) + bias_in[pl.ds(n, 1), :], 0.0)
            fin[:, n * BS : (n + 1) * BS] = value.astype(BF16)

        @pl.when(away)
        def _():
            back(h, s).start()

    reduce_scatter(
        other, near_y, result_sum(core), result_sum(1 - core), sent, got_b, out1, in1_b, out2, in2_b, sems_b,
        finish_result, lambda stage: None,
    )

    @pl.when(away)
    def _():
        for s in range(2):
            for h in range(2):
                back(h, s).wait()
        for copy in swaps():
            copy.wait_send()

    @pl.when(jnp.logical_not(away))
    def _():
        out[...] = fin[...]

    @pl.loop(0, ORDER)
    def _(i):
        given(i).wait_send()

    for copy in (*small, *copies):
        copy.wait_send()
    ring1.end()
    ring2.end()


ANY = pl.BlockSpec(memory_space=pl.ANY)
VMEM = pl.BlockSpec(memory_space=pltpu.VMEM)


def on_device(acts, act_mask, w1, cols1, bias1, mask2, w2, cols2, bias2):
    n = acts.shape[0]
    dma = pltpu.SemaphoreType.DMA
    whole = pltpu.VMEM((RING, CHUNKS, ENTRIES, BS, BS), BF16)
    tiles = lambda *count: pltpu.VMEM((*count, BS, BS), BF16)
    table_v, table = pltpu.VMEM((16, 128), I32), pltpu.SMEM((16, 128), I32)
    arrivals = (tiles(4, UNITS), tiles(2, 2, 2, PART), tiles(2, 2, PART))
    return pl.pallas_call(
        kernel,
        out_shape=jax.ShapeDtypeStruct((n, UNITS * BS), BF16),
        in_specs=[ANY, ANY, ANY, *[VMEM] * 6],
        out_specs=VMEM,
        scratch_shapes=[
            whole,
            whole,
            pltpu.VMEM((NOTHING + 1, 2 * n, BS), F32),
            pltpu.VMEM((ORDER, 2 * n, BS), BF16),
            tiles(UNITS),
            pltpu.VMEM((64, n), I32),
            pltpu.VMEM((2, 64, n), I32),
            pltpu.VMEM((ENTRIES, 64), I32),
            pltpu.VMEM((UNITS, BS), F32),
            table_v,
            table_v,
            table,
            table,
            tiles(4, UNITS),
            tiles(2, 2, 2, PART),
            tiles(2, 2, PART),
            *arrivals,
            *arrivals,
            pltpu.VMEM((n, UNITS * BS), BF16),
            dma((CHUNKS,)),
            dma((2, 2, HOPS)),
            dma((2, 2, HOPS)),
            dma((ORDER,)),
            dma((2, ORDER)),
            dma((2, 2)),
            dma((2, 3)),
            dma((2,)),
            dma((2, 28)),
            dma((2, 28)),
            dma((2, 12)),
            dma((2, 4)),
        ],
        compiler_params=pltpu.CompilerParams(collective_id=0, has_side_effects=True, vmem_limit_bytes=67_043_328),
        name="layers",
    )(
        w1, w2, acts, act_mask.T, mask2.T, cols1.T, cols2.T, bias1.reshape(COLUMNS, BS), bias2.reshape(UNITS, BS)
    )


def solution(mesh):
    finer = Mesh(mesh.devices.reshape(2, 2, mesh.shape["col"], RING, 2), AXES)
    in_specs = (
        P(DEPTH, ROW),
        P(DEPTH, ROW),
        P((*ROW, *DEPTH), "y", None, None),
        P(ROW, "y"),
        P("y"),
        P(DEPTH, "y"),
        P(("y", *DEPTH), ROW, None, None),
        P("y", ROW),
        P((*ROW, "y")),
    )
    out_specs = P(DEPTH, (*ROW, "y"))
    return jax.shard_map(on_device, mesh=finer, in_specs=in_specs, out_specs=out_specs, check_vma=False)
```

time: 907 us -> 203 us (0.22); the launches traced: 896 us -> 203 us
  waiting for transfers between devices: 433 us -> 0 us
  other arithmetic: 208 us -> 0 us
  Pallas kernels: 0 us -> 201 us
  matrix products: 99.2 us -> 0 us
  local copies, waits for them, and re-layouts: 76.5 us -> 1.88 us
  blocking collectives: 54.2 us -> 0 us
  between operations: 13.2 us -> 0.01 us
  starting transfers between devices: 11.1 us -> 0 us
    all_gather x3 -> x0, waiting for transfers between devices: 290 us -> none  [the longest x2 214 us: whole_of(): result = lax.all_gather(result, axes[number], axis=dim, tiled=True)]
    pallas_call x0 -> x1, Pallas kernels: none -> 201 us  [on_device(): pl.pallas_call(kernel, out_shape=jax.ShapeDtypeStruct((n, UNITS * BS), BF...]
    scatter-add x32 -> x0, other arithmetic: 199 us -> none  [advance(): return total.at[:, wanted.reshape(-1)].add(flat_product)]
    all_to_all x2 -> x0, waiting for transfers between devices: 142 us -> none  [the longest x1 141 us: summed_on_arrival(): parts = lax.all_to_all(split_up(x, dim, count), axis, 0, 0, tiled=True)]
    dot_general x32 -> x0, matrix products: 99.2 us -> none  [advance(): jnp.einsum('tws,wish->twih', incoming_rows, block_list, preferred_element...]
    reshape x64 -> x0, local copies, waits for them, and re-layouts: 64.1 us -> none  [the longest x32 61.5 us: advance(): flat_product = product.reshape(product.shape[0], -1, product.shape[-1])]
    all_to_all x1 -> x0, blocking collectives: 54.2 us -> none  [summed_on_arrival(): parts = lax.all_to_all(split_up(x, dim, count), axis, 0, 0, tiled=True)]
    all_to_all x2 -> x0, starting transfers between devices: 11.1 us -> none  [the longest x1 5.66 us: summed_on_arrival(): parts = lax.all_to_all(split_up(x, dim, count), axis, 0, 0, tiled=True)]
  transfers between devices with their start and end apart: 5 -> 0, of which waited for: 5 -> 0; matrix products, arithmetic and copies ran while one was open for 22% -> 0% of each run, Pallas kernels for 0% -> 0%
where the time goes in v3:
time: 203 us
  Pallas kernels  201 us (99%)
    pallas_call x1, Pallas kernels, on_device(): pl.pallas_call(kernel, out_shape=jax.ShapeDtypeStruct((n, UNITS * BS), BF...  201 us

profile of v3, /device:TPU:1, one launch (start us, length us, event | category | flops | bytes accessed | tf_op | source)
XLA Modules:
  0.0 202.8 jit_solution(1102456077293781405)
XLA Ops:
  0.0 200.9 %layers.1 = bf16[128,2048]{1,0:T(8,128)(2,1)} custom-call(bf16[4,8,128,128]{3,2,1,0:T(8,128)(2,1)} %w1.1, bf16[4,8,128,128]{3,2,1,0:T(8,128)(2,1)} %w2.1, bf16[128,8192]{1,0:T(8,128)(2,1)} %acts.1, s32[64,128]{1,0:T(8,128)} %bitcast.6, s32[64,128]{1,0:T(8,128)} %bitcast.7, s32[8,64]{1,0:T(8,128)} %bitcast.10, s32[8,64]{1,0:T(8,128)} %bitcast.11, ...), custom_call_target="tpu_custom_call" | custom-call | tf_op jit(solution)/shard_map/layers/pallas_call | solution.py:466
  200.9 1.9 copy.11

commit v4 on v3

--- a/solution.py
+++ b/solution.py
@@ -54,9 +54,11 @@
         ref = self.whole.at[slot, c]
         return remote(ref, ref, self.sems.at[0, way, n], self.sems.at[1, way, n], self.to[way])
 
-    def start(self):
+    def start_loads(self):
         for c in range(CHUNKS):
             self.load(c).start()
+
+    def start(self):
         for c in range(CHUNKS):
             self.load(c).wait()
             for way in range(2):
@@ -154,7 +156,7 @@
 PART = 4
 
 
-def reduce_scatter(other, near, mine, theirs, sent, got, out1, in1, out2, in2, sems, finish, between):
+def reduce_scatter(other, near, last, mine, theirs, sent, got, out1, in1, out2, in2, sems, keep, finish, between):
     def start(n, src, dst, device):
         copy = remote(src, dst, sems.at[0, n], sems.at[1, n], device)
         copy.start()
@@ -163,24 +165,23 @@
     def unit(h, s, c):
         return (2 * h + s) * PART + c
 
-    exchanged, firsts, seconds = {}, {}, {}
-    order = [(2, 0), (2, 1), (1, 0), (3, 1), (3, 0), (1, 1), (0, 0), (0, 1)]
-    for s in range(2):
-        for g, h in order:
-
-            @pl.loop(0, PART)
-            def _(c):
-                n = unit(h, s, c)
-                sent[g, n] = theirs(g, n).astype(BF16)
-
-            ref = pl.ds(unit(h, s, 0), PART)
-            exchanged[g, h, s] = start(len(exchanged), sent.at[g, ref], got.at[g, ref], other)
-    between(0)
-
     def both(g, h, s, c):
         n = unit(h, s, c)
         return mine(g, n) + got[g, n].astype(F32)
 
+    exchanged, firsts, seconds = {}, {}, {}
+
+    def exchange(s):
+        for g, h in [(1, 0), (3, 1), (2, 0), (2, 1), (0, 0), (0, 1), (3, 0), (1, 1)]:
+            ref = sent(g, unit(h, s, 0))
+
+            @pl.loop(0, PART)
+            def _(c):
+                ref[c] = theirs(g, unit(h, s, c)).astype(BF16)
+
+            place = got.at[g, pl.ds(unit(h, s, 0), PART)]
+            exchanged[g, h, s] = start(len(exchanged), ref, place, other)
+
     def first(s, step):
         for h in range(2):
             g = FIRST[h][step]
@@ -203,34 +204,37 @@
             def _(c):
                 out2[h, s, c] = (both(g, h, s, c) + in1[h, 0, s, c].astype(F32)).astype(BF16)
 
-            seconds[h, s] = start(24 + 2 * s + h, out2.at[h, s], in2.at[h, s], near[1 - h])
-
-    first(0, 0)
-    first(0, 1)
-    first(1, 0)
-    between(1)
-    second(0)
-    first(1, 1)
-    second(1)
-    between(2)
-    for s in range(2):
+            seconds[h, s] = start(24 + 2 * s + h, out2.at[h, s], in2.at[h, s], last[1 - h])
+
+    def own(s):
         for h in range(2):
             exchanged[0, h, s].wait_recv()
             firsts[h, s, 1].wait_recv()
+            keep(h, s, lambda c: both(0, h, s, c) + in1[h, 1, s, c].astype(F32))
+
+    for s in range(2):
+        exchange(s)
+        first(s, 1)
+        first(s, 0)
+    between(0)
+    for s in range(2):
+        own(s)
+        second(s)
+    between(1)
+    for s in range(2):
+        for h in range(2):
             seconds[h, s].wait_recv()
-            finish(
-                h, s, lambda c: both(0, h, s, c) + in1[h, 1, s, c].astype(F32) + in2[h, s, c].astype(F32)
-            )
+            finish(h, s, lambda c: in2[h, s, c].astype(F32))
     for copy in [*exchanged.values(), *firsts.values(), *seconds.values()]:
         copy.wait_send()
 
 
 def kernel(
     w1, w2, acts, act_mask, mask2, columns1, columns2, bias1, bias2, out,
-    whole1, whole2, sums, x0, live, mask_taken, masks2, columns_in, bias_in, table_v1, table_v2, table1, table2,
-    sent, out1, out2, got_a, in1_a, in2_a, got_b, in1_b, in2_b, fin,
+    whole1, whole2, sums, x0, live, mask_taken, masks2, columns_in, table_v1, table_v2, table1, table2,
+    out1, out2, got_a, in1_a, in2_a, got_b, in1_b, in2_b, kept,
     load_sems, ring1_sems, ring2_sems, mine_sems, taken_sems, small_sems, swap_sems, table_sems,
-    sems_a, sems_b, spread_sems, back_sems,
+    sems_a, sems_b, spread_sems, kept_sems,
 ):
     xh, core, y, z, xl = (lax.axis_index(a) for a in AXES)
     x = xh * 2 + xl
@@ -240,14 +244,31 @@
     near_x = ({"xl": 1 - xl}, {"xh": 1 - xh, "xl": 1 - xl})
     chips = (xh * 2 + 1 - xl, 3 - x)
     near_y = ({"y": y + 1 - 2 * lax.rem(y, 2)}, {"y": 3 - y})
+    last_y = tuple({**near, "core": xl, "xl": core} for near in near_y)
     beside = near_x[0]
     ring1 = Ring(w1, whole1, z, load_sems, ring1_sems)
     ring2 = Ring(w2, whole2, z, load_sems, ring2_sems)
-    greet((*ring1.to, other, home, *near_x, *near_y))
 
     def rows_of(c):
         return pl.ds(pl.multiple_of(c * BS, BS), BS)
 
+    def block(i, parity):
+        b = i // CHUNKS * 8 + parity * CHUNKS + lax.rem(i, CHUNKS)
+        return acts.at[:, pl.ds(pl.multiple_of(b * BS, BS), BS)]
+
+    def given(i):
+        return remote(block(i, 1 - xl), x0.at[i, rows_of(xl)], taken_sems.at[0, i], taken_sems.at[1, i], beside)
+
+    def own(i):
+        return pltpu.make_async_copy(block(i, xl), x0.at[i, rows_of(xl)], mine_sems.at[i])
+
+    ring1.start_loads()
+
+    @pl.loop(0, ORDER)
+    def _(i):
+        own(i).start()
+
+    greet((*ring1.to, other, home, *near_x, *near_y, *last_y))
     ring1.start()
     small = [
         remote(act_mask, mask_taken, small_sems.at[0, 0], small_sems.at[1, 0], beside),
@@ -256,28 +277,17 @@
     for copy in small:
         copy.start()
 
-    def block(i, parity):
-        b = i // CHUNKS * 8 + parity * CHUNKS + lax.rem(i, CHUNKS)
-        return acts.at[:, pl.ds(pl.multiple_of(b * BS, BS), BS)]
-
-    def given(i):
-        return remote(block(i, 1 - xl), x0.at[i, rows_of(xl)], taken_sems.at[0, i], taken_sems.at[1, i], beside)
-
-    def own(i):
-        return pltpu.make_async_copy(block(i, xl), x0.at[i, rows_of(xl)], mine_sems.at[i])
-
     @pl.loop(0, ORDER)
     def _(i):
         given(i).start()
-        own(i).start()
-
-    moves = ((columns2, columns_in), (bias2, bias_in), (w2, whole2.at[z]))
+
+    moves = ((columns2, columns_in), (w2, whole2.at[z]))
 
     def swaps():
         return [remote(src, dst, swap_sems.at[0, n], swap_sems.at[1, n], home) for n, (src, dst) in enumerate(moves)]
 
     def stay():
-        return pltpu.make_async_copy(w2, whole2.at[z], swap_sems.at[0, 2])
+        return pltpu.make_async_copy(w2, whole2.at[z], swap_sems.at[0, 1])
 
     @pl.when(away)
     def _():
@@ -288,7 +298,6 @@
     def _():
         stay().start()
         columns_in[...] = columns2[...]
-        bias_in[...] = bias2[...]
 
     masks2[xl] = mask2[...]
     write_tables(columns1, y * COLUMNS, z, xl, table_v1)
@@ -350,6 +359,10 @@
     to_scalars2 = pltpu.make_async_copy(table_v2, table2, table_sems.at[1])
     to_scalars2.start()
     use_arrived(x0, ring1, sums, table1, 12, HOPS, False)
+    ring1.end()
+
+    def sent(g, n):
+        return whole1.at[g // 2, g % 2 * 2 + n // 8, pl.ds(n % 8, PART)]
 
     def hidden_sum(parity):
         def unit(g, n):
@@ -370,22 +383,24 @@
         copies.append(copy)
         return copy
 
-    def finish_hidden(h, s, total):
+    def keep_hidden(h, s, total):
+        @pl.loop(0, PART)
+        def _(c):
+            kept[0, h, s, c] = total(c)
+
+    def finish_hidden(h, s, rest):
         for c in range(PART):
             n = (2 * h + s) * PART + c
             j = (x * 2 + n // 8) * 8 + core * 4 + n // 2 % 4
-            value = jnp.maximum(total(c) + bias1[pl.ds(j, 1), :], 0.0) * live[n].astype(F32)
+            total = kept[0, h, s, c] + rest(c)
+            value = jnp.maximum(total + bias1[pl.ds(j, 1), :], 0.0) * live[n].astype(F32)
             x0[x * 8 + n // 2, pl.ds(n % 2 * BS, BS), :] = value.astype(BF16)
         for to in (1 - h, h):
             spreads[h, s, to] = spread(x, h, s, to)
 
-    def between_hidden(stage):
-        if stage > 0:
-            ring2.pumps(stage - 1, stage)
-
     reduce_scatter(
-        other, near_x, hidden_sum(core), hidden_sum(1 - core), sent, got_a, out1, in1_a, out2, in2_a, sems_a,
-        finish_hidden, between_hidden,
+        other, near_x, near_x, hidden_sum(core), hidden_sum(1 - core), sent, got_a, out1, in1_a, out2, in2_a, sems_a,
+        keep_hidden, finish_hidden, lambda stage: ring2.pumps(stage, stage + 1),
     )
     ring2.pumps(2, 4)
     last = []
@@ -411,36 +426,41 @@
 
         return unit
 
-    def back(h, s):
-        ref, n = pl.ds((2 * h + s) * PART * BS, PART * BS), 2 * h + s
-        return remote(fin.at[:, ref], out.at[:, ref], back_sems.at[0, n], back_sems.at[1, n], home)
-
-    def finish_result(h, s, total):
+    def send_kept(h, s):
+        n = 2 * h + s
+        return remote(kept.at[0, h, s], kept.at[1, h, s], kept_sems.at[0, n], kept_sems.at[1, n], home)
+
+    def keep_result(h, s, total):
+        @pl.loop(0, PART)
+        def _(c):
+            kept[0, h, s, c] = total(c)
+
+        @pl.when(away)
+        def _():
+            send_kept(h, s).start()
+
+    def finish_result(h, s, rest):
+        @pl.when(away)
+        def _():
+            send_kept(h, s).wait_recv()
+
         for c in range(PART):
             n = (2 * h + s) * PART + c
-            value = jnp.maximum(total(c) + bias_in[pl.ds(n, 1), :], 0.0)
-            fin[:, n * BS : (n + 1) * BS] = value.astype(BF16)
-
-        @pl.when(away)
-        def _():
-            back(h, s).start()
+            total = kept[lax.rem(core + xl, 2), h, s, c] + rest(c)
+            out[:, n * BS : (n + 1) * BS] = jnp.maximum(total + bias2[pl.ds(n, 1), :], 0.0).astype(BF16)
 
     reduce_scatter(
-        other, near_y, result_sum(core), result_sum(1 - core), sent, got_b, out1, in1_b, out2, in2_b, sems_b,
-        finish_result, lambda stage: None,
+        other, near_y, last_y, result_sum(core), result_sum(1 - core), sent, got_b, out1, in1_b, out2, in2_b, sems_b,
+        keep_result, finish_result, lambda stage: None,
     )
 
     @pl.when(away)
     def _():
-        for s in range(2):
-            for h in range(2):
-                back(h, s).wait()
+        for h in range(2):
+            for s in range(2):
+                send_kept(h, s).wait_send()
         for copy in swaps():
             copy.wait_send()
-
-    @pl.when(jnp.logical_not(away))
-    def _():
-        out[...] = fin[...]
 
     @pl.loop(0, ORDER)
     def _(i):
@@ -448,7 +468,6 @@
 
     for copy in (*small, *copies):
         copy.wait_send()
-    ring1.end()
     ring2.end()
 
 
@@ -477,24 +496,22 @@
             pltpu.VMEM((64, n), I32),
             pltpu.VMEM((2, 64, n), I32),
             pltpu.VMEM((ENTRIES, 64), I32),
-            pltpu.VMEM((UNITS, BS), F32),
             table_v,
             table_v,
             table,
             table,
-            tiles(4, UNITS),
             tiles(2, 2, 2, PART),
             tiles(2, 2, PART),
             *arrivals,
             *arrivals,
-            pltpu.VMEM((n, UNITS * BS), BF16),
+            pltpu.VMEM((2, 2, 2, PART, BS, BS), F32),
             dma((CHUNKS,)),
             dma((2, 2, HOPS)),
             dma((2, 2, HOPS)),
             dma((ORDER,)),
             dma((2, ORDER)),
             dma((2, 2)),
-            dma((2, 3)),
+            dma((2, 2)),
             dma((2,)),
             dma((2, 28)),
             dma((2, 28)),

time: 203 us -> 202 us (level)
  no operation moved by 1% of the time
where the time goes in v4:
time: 202 us
  Pallas kernels  200 us (99%)
    pallas_call x1, Pallas kernels, on_device(): pl.pallas_call(kernel, out_shape=jax.ShapeDtypeStruct((n, UNITS * BS), BF...  200 us

profile of v4, /device:TPU:1, one launch (start us, length us, event | category | flops | bytes accessed | tf_op | source)
XLA Modules:
  0.0 201.7 jit_solution(11163698436750684182)
XLA Ops:
  0.0 199.8 %layers.1 = bf16[128,2048]{1,0:T(8,128)(2,1)} custom-call(bf16[4,8,128,128]{3,2,1,0:T(8,128)(2,1)} %w1.1, bf16[4,8,128,128]{3,2,1,0:T(8,128)(2,1)} %w2.1, bf16[128,8192]{1,0:T(8,128)(2,1)} %acts.1, s32[64,128]{1,0:T(8,128)} %bitcast.6, s32[64,128]{1,0:T(8,128)} %bitcast.7, s32[8,64]{1,0:T(8,128)} %bitcast.10, s32[8,64]{1,0:T(8,128)} %bitcast.11, ...), custom_call_target="tpu_custom_call" | custom-call | tf_op jit(solution)/shard_map/layers/pallas_call | solution.py:485
  199.8 1.9 copy.11

commit v5 on v4

--- a/solution.py
+++ b/solution.py
@@ -142,10 +142,9 @@
 def use_arrived(x_ref, ring, sums, table, first, last, pumped):
     @pl.loop(first, last)
     def _(n):
-        if not pumped:
-            for way in range(2):
+        for way in range(2):
+            if not pumped:
                 ring.pump(way, n)
-        for way in range(2):
             slot, c = ring.chunk(way, n, 1)
             use(x_ref, ring, sums, table, slot, c, CHUNKS + 2 * n + way)
 
@@ -221,18 +220,20 @@
         own(s)
         second(s)
     between(1)
+    for copy in (*exchanged.values(), *firsts.values()):
+        copy.wait_send()
     for s in range(2):
         for h in range(2):
             seconds[h, s].wait_recv()
             finish(h, s, lambda c: in2[h, s, c].astype(F32))
-    for copy in [*exchanged.values(), *firsts.values(), *seconds.values()]:
+    for copy in seconds.values():
         copy.wait_send()
 
 
 def kernel(
     w1, w2, acts, act_mask, mask2, columns1, columns2, bias1, bias2, out,
     whole1, whole2, sums, x0, live, mask_taken, masks2, columns_in, table_v1, table_v2, table1, table2,
-    out1, out2, got_a, in1_a, in2_a, got_b, in1_b, in2_b, kept,
+    out1, out2, got_a, in1_a, in2_a, got_b, in1_b, in2_b, kept, kept_out, kept_in,
     load_sems, ring1_sems, ring2_sems, mine_sems, taken_sems, small_sems, swap_sems, table_sems,
     sems_a, sems_b, spread_sems, kept_sems,
 ):
@@ -386,13 +387,13 @@
     def keep_hidden(h, s, total):
         @pl.loop(0, PART)
         def _(c):
-            kept[0, h, s, c] = total(c)
+            kept[h, s, c] = total(c)
 
     def finish_hidden(h, s, rest):
         for c in range(PART):
             n = (2 * h + s) * PART + c
             j = (x * 2 + n // 8) * 8 + core * 4 + n // 2 % 4
-            total = kept[0, h, s, c] + rest(c)
+            total = kept[h, s, c] + rest(c)
             value = jnp.maximum(total + bias1[pl.ds(j, 1), :], 0.0) * live[n].astype(F32)
             x0[x * 8 + n // 2, pl.ds(n % 2 * BS, BS), :] = value.astype(BF16)
         for to in (1 - h, h):
@@ -428,16 +429,35 @@
 
     def send_kept(h, s):
         n = 2 * h + s
-        return remote(kept.at[0, h, s], kept.at[1, h, s], kept_sems.at[0, n], kept_sems.at[1, n], home)
+        return remote(kept_out.at[h, s], kept_in.at[h, s], kept_sems.at[0, n], kept_sems.at[1, n], home)
 
     def keep_result(h, s, total):
         @pl.loop(0, PART)
         def _(c):
-            kept[0, h, s, c] = total(c)
+            value = total(c)
+            kept[h, s, c] = value
+            kept_out[h, s, c] = value.astype(BF16)
 
         @pl.when(away)
         def _():
             send_kept(h, s).start()
+
+    def sent_all(stage):
+        if stage > 0:
+            return
+
+        @pl.loop(0, ORDER)
+        def _(i):
+            given(i).wait_send()
+
+        @pl.when(away)
+        def _():
+            for copy in swaps():
+                copy.wait_send()
+
+        for copy in (*small, *copies):
+            copy.wait_send()
+        ring2.end()
 
     def finish_result(h, s, rest):
         @pl.when(away)
@@ -446,12 +466,12 @@
 
         for c in range(PART):
             n = (2 * h + s) * PART + c
-            total = kept[lax.rem(core + xl, 2), h, s, c] + rest(c)
+            total = jnp.where(away, kept_in[h, s, c].astype(F32), kept[h, s, c]) + rest(c)
             out[:, n * BS : (n + 1) * BS] = jnp.maximum(total + bias2[pl.ds(n, 1), :], 0.0).astype(BF16)
 
     reduce_scatter(
         other, near_y, last_y, result_sum(core), result_sum(1 - core), sent, got_b, out1, in1_b, out2, in2_b, sems_b,
-        keep_result, finish_result, lambda stage: None,
+        keep_result, finish_result, sent_all,
     )
 
     @pl.when(away)
@@ -459,16 +479,6 @@
         for h in range(2):
             for s in range(2):
                 send_kept(h, s).wait_send()
-        for copy in swaps():
-            copy.wait_send()
-
-    @pl.loop(0, ORDER)
-    def _(i):
-        given(i).wait_send()
-
-    for copy in (*small, *copies):
-        copy.wait_send()
-    ring2.end()
 
 
 ANY = pl.BlockSpec(memory_space=pl.ANY)
@@ -504,7 +514,9 @@
             tiles(2, 2, PART),
             *arrivals,
             *arrivals,
-            pltpu.VMEM((2, 2, 2, PART, BS, BS), F32),
+            pltpu.VMEM((2, 2, PART, BS, BS), F32),
+            tiles(2, 2, PART),
+            tiles(2, 2, PART),
             dma((CHUNKS,)),
             dma((2, 2, HOPS)),
             dma((2, 2, HOPS)),

time: 202 us -> 198 us (0.980)
  Pallas kernels: 200 us -> 196 us
    pallas_call x1, Pallas kernels: 200 us -> 196 us  [on_device(): pl.pallas_call(kernel, out_shape=jax.ShapeDtypeStruct((n, UNITS * BS), BF...]
where the time goes in v5:
time: 198 us
  Pallas kernels  196 us (99%)
    pallas_call x1, Pallas kernels, on_device(): pl.pallas_call(kernel, out_shape=jax.ShapeDtypeStruct((n, UNITS * BS), BF...  196 us

profile of v5, /device:TPU:1, one launch (start us, length us, event | category | flops | bytes accessed | tf_op | source)
XLA Modules:
  0.0 197.6 jit_solution(2686363162495430061)
XLA Ops:
  0.0 195.8 %layers.1 = bf16[128,2048]{1,0:T(8,128)(2,1)} custom-call(bf16[4,8,128,128]{3,2,1,0:T(8,128)(2,1)} %w1.1, bf16[4,8,128,128]{3,2,1,0:T(8,128)(2,1)} %w2.1, bf16[128,8192]{1,0:T(8,128)(2,1)} %acts.1, s32[64,128]{1,0:T(8,128)} %bitcast.6, s32[64,128]{1,0:T(8,128)} %bitcast.7, s32[8,64]{1,0:T(8,128)} %bitcast.10, s32[8,64]{1,0:T(8,128)} %bitcast.11, ...), custom_call_target="tpu_custom_call" | custom-call | tf_op jit(solution)/shard_map/layers/pallas_call | solution.py:495
  195.8 1.9 copy.11

commit v6 on v5

--- a/solution.py
+++ b/solution.py
@@ -231,10 +231,10 @@
 
 
 def kernel(
-    w1, w2, acts, act_mask, mask2, columns1, columns2, bias1, bias2, out,
-    whole1, whole2, sums, x0, live, mask_taken, masks2, columns_in, table_v1, table_v2, table1, table2,
+    w1, w2, acts, act_mask, mask2, columns1, columns2, bias1_in, bias2_in, out,
+    whole1, whole2, sums, x0, live, mask_own, mask_taken, masks2, columns_own, columns_in, bias1, bias2, table_v1, table_v2, table1, table2,
     out1, out2, got_a, in1_a, in2_a, got_b, in1_b, in2_b, kept, kept_out, kept_in,
-    load_sems, ring1_sems, ring2_sems, mine_sems, taken_sems, small_sems, swap_sems, table_sems,
+    load_sems, ring1_sems, ring2_sems, fetch_sems, mine_sems, taken_sems, small_sems, swap_sems, table_sems,
     sems_a, sems_b, spread_sems, kept_sems,
 ):
     xh, core, y, z, xl = (lax.axis_index(a) for a in AXES)
@@ -264,13 +264,22 @@
         return pltpu.make_async_copy(block(i, xl), x0.at[i, rows_of(xl)], mine_sems.at[i])
 
     ring1.start_loads()
-
-    @pl.loop(0, ORDER)
-    def _(i):
-        own(i).start()
-
-    greet((*ring1.to, other, home, *near_x, *near_y, *last_y))
+    greet((*ring1.to, other, home, *near_x, *near_y))
     ring1.start()
+    fetches = [
+        pltpu.make_async_copy(src, dst, fetch_sems.at[n])
+        for n, (src, dst) in enumerate(
+            (
+                (columns1, columns_own),
+                (act_mask, mask_own),
+                (mask2, masks2.at[xl]),
+                (bias1_in, bias1),
+                (bias2_in, bias2),
+            )
+        )
+    ]
+    for copy in fetches:
+        copy.start()
     small = [
         remote(act_mask, mask_taken, small_sems.at[0, 0], small_sems.at[1, 0], beside),
         remote(mask2, masks2.at[xl], small_sems.at[0, 1], small_sems.at[1, 1], beside),
@@ -281,6 +290,7 @@
     @pl.loop(0, ORDER)
     def _(i):
         given(i).start()
+        own(i).start()
 
     moves = ((columns2, columns_in), (w2, whole2.at[z]))
 
@@ -288,7 +298,7 @@
         return [remote(src, dst, swap_sems.at[0, n], swap_sems.at[1, n], home) for n, (src, dst) in enumerate(moves)]
 
     def stay():
-        return pltpu.make_async_copy(w2, whole2.at[z], swap_sems.at[0, 1])
+        return [pltpu.make_async_copy(src, dst, swap_sems.at[0, n]) for n, (src, dst) in enumerate(moves)]
 
     @pl.when(away)
     def _():
@@ -297,11 +307,12 @@
 
     @pl.when(jnp.logical_not(away))
     def _():
-        stay().start()
-        columns_in[...] = columns2[...]
-
-    masks2[xl] = mask2[...]
-    write_tables(columns1, y * COLUMNS, z, xl, table_v1)
+        for copy in stay():
+            copy.start()
+
+    for copy in fetches:
+        copy.wait()
+    write_tables(columns_own, y * COLUMNS, z, xl, table_v1)
     sums[NOTHING] = jnp.zeros(sums.shape[1:], F32)
 
     def by_rows(mask):
@@ -320,7 +331,7 @@
     def _(i):
         own(i).wait()
 
-    masked(act_mask, rows_of(xl))
+    masked(mask_own, rows_of(xl))
     to_scalars1 = pltpu.make_async_copy(table_v1, table1, table_sems.at[0])
     to_scalars1.start()
     ring1.pumps(0, 3)
@@ -352,7 +363,8 @@
 
     @pl.when(jnp.logical_not(away))
     def _():
-        stay().wait()
+        for copy in stay():
+            copy.wait()
 
     write_tables(columns_in, x * COLUMNS, z, core, table_v2)
     use_arrived(x0, ring1, sums, table1, 5, 12, False)
@@ -419,7 +431,20 @@
 
     use_own(x0, ring2, sums, table2)
     use_arrived(x0, ring2, sums, table2, 0, 6, True)
-    use_arrived(x0, ring2, sums, table2, 6, HOPS, False)
+    use_arrived(x0, ring2, sums, table2, 6, 10, False)
+
+    @pl.loop(0, ORDER)
+    def _(i):
+        given(i).wait_send()
+
+    @pl.when(away)
+    def _():
+        for copy in swaps():
+            copy.wait_send()
+
+    for copy in (*small, *copies):
+        copy.wait_send()
+    use_arrived(x0, ring2, sums, table2, 10, HOPS, False)
 
     def result_sum(half):
         def unit(g, n):
@@ -442,23 +467,6 @@
         def _():
             send_kept(h, s).start()
 
-    def sent_all(stage):
-        if stage > 0:
-            return
-
-        @pl.loop(0, ORDER)
-        def _(i):
-            given(i).wait_send()
-
-        @pl.when(away)
-        def _():
-            for copy in swaps():
-                copy.wait_send()
-
-        for copy in (*small, *copies):
-            copy.wait_send()
-        ring2.end()
-
     def finish_result(h, s, rest):
         @pl.when(away)
         def _():
@@ -471,7 +479,7 @@
 
     reduce_scatter(
         other, near_y, last_y, result_sum(core), result_sum(1 - core), sent, got_b, out1, in1_b, out2, in2_b, sems_b,
-        keep_result, finish_result, sent_all,
+        keep_result, finish_result, lambda stage: None,
     )
 
     @pl.when(away)
@@ -479,6 +487,8 @@
         for h in range(2):
             for s in range(2):
                 send_kept(h, s).wait_send()
+
+    ring2.end()
 
 
 ANY = pl.BlockSpec(memory_space=pl.ANY)
@@ -495,7 +505,7 @@
     return pl.pallas_call(
         kernel,
         out_shape=jax.ShapeDtypeStruct((n, UNITS * BS), BF16),
-        in_specs=[ANY, ANY, ANY, *[VMEM] * 6],
+        in_specs=[ANY] * 9,
         out_specs=VMEM,
         scratch_shapes=[
             whole,
@@ -504,8 +514,12 @@
             pltpu.VMEM((ORDER, 2 * n, BS), BF16),
             tiles(UNITS),
             pltpu.VMEM((64, n), I32),
+            pltpu.VMEM((64, n), I32),
             pltpu.VMEM((2, 64, n), I32),
             pltpu.VMEM((ENTRIES, 64), I32),
+            pltpu.VMEM((ENTRIES, 64), I32),
+            pltpu.VMEM((COLUMNS, BS), F32),
+            pltpu.VMEM((UNITS, BS), F32),
             table_v,
             table_v,
             table,
@@ -520,6 +534,7 @@
             dma((CHUNKS,)),
             dma((2, 2, HOPS)),
             dma((2, 2, HOPS)),
+            dma((5,)),
             dma((ORDER,)),
             dma((2, ORDER)),
             dma((2, 2)),

time: 198 us -> 197 us (level)
  no operation moved by 1% of the time
where the time goes in v6:
time: 197 us
  Pallas kernels  195 us (99%)
    pallas_call x1, Pallas kernels, on_device(): pl.pallas_call(kernel, out_shape=jax.ShapeDtypeStruct((n, UNITS * BS), BF...  195 us

profile of v6, /device:TPU:1, one launch (start us, length us, event | category | flops | bytes accessed | tf_op | source)
XLA Modules:
  0.0 196.5 jit_solution(11203244082594670567)
XLA Ops:
  0.0 194.6 %layers.1 = bf16[128,2048]{1,0:T(8,128)(2,1)} custom-call(bf16[4,8,128,128]{3,2,1,0:T(8,128)(2,1)} %w1.1, bf16[4,8,128,128]{3,2,1,0:T(8,128)(2,1)} %w2.1, bf16[128,8192]{1,0:T(8,128)(2,1)} %acts.1, s32[64,128]{1,0:T(8,128)} %bitcast.6, s32[64,128]{1,0:T(8,128)} %bitcast.7, s32[8,64]{1,0:T(8,128)} %bitcast.10, s32[8,64]{1,0:T(8,128)} %bitcast.11, ...), custom_call_target="tpu_custom_call" | custom-call | tf_op jit(solution)/shard_map/layers/pallas_call | solution.py:505
  194.7 1.9 copy.11

commit v7 on v6

--- a/solution.py
+++ b/solution.py
@@ -39,8 +39,9 @@
 
 
 class Ring:
-    def __init__(self, shard, whole, z, load_sems, sems):
-        self.shard, self.whole, self.z, self.load_sems, self.sems = shard, whole, z, load_sems, sems
+    def __init__(self, shard, whole, z, load_sems, sems, sent_sem):
+        self.shard, self.whole, self.z = shard, whole, z
+        self.load_sems, self.sems, self.sent_sem = load_sems, sems, sent_sem
         self.to = ({"z": lax.rem(z + 1, RING)}, {"z": lax.rem(z + RING - 1, RING)})
 
     def chunk(self, way, n, steps):
@@ -52,7 +53,7 @@
     def hop(self, way, n):
         slot, c = self.chunk(way, n, 0)
         ref = self.whole.at[slot, c]
-        return remote(ref, ref, self.sems.at[0, way, n], self.sems.at[1, way, n], self.to[way])
+        return remote(ref, ref, self.sent_sem, self.sems.at[way, n], self.to[way])
 
     def start_loads(self):
         for c in range(CHUNKS):
@@ -92,10 +93,8 @@
                 self.pump(way, n)
 
     def end(self):
-        @pl.loop(0, HOPS)
-        def _(n):
-            for way in range(2):
-                self.hop(way, n).wait_send()
+        ref = self.whole.at[pl.ds(0, 2 * HOPS // CHUNKS)]
+        remote(ref, ref, self.sent_sem, self.sems.at[0, 0], self.to[0]).wait_send()
 
 
 def write_tables(columns_ref, base, z, parity, table_ref):
@@ -155,9 +154,9 @@
 PART = 4
 
 
-def reduce_scatter(other, near, last, mine, theirs, sent, got, out1, in1, out2, in2, sems, keep, finish, between):
-    def start(n, src, dst, device):
-        copy = remote(src, dst, sems.at[0, n], sems.at[1, n], device)
+def reduce_scatter(other, near, last, mine, theirs, sent, got, out1, in1, out2, in2, sems, sent_sems, keep, finish, between):
+    def start(n, kind, src, dst, device):
+        copy = remote(src, dst, sent_sems.at[kind], sems.at[n], device)
         copy.start()
         return copy
 
@@ -179,7 +178,7 @@
                 ref[c] = theirs(g, unit(h, s, c)).astype(BF16)
 
             place = got.at[g, pl.ds(unit(h, s, 0), PART)]
-            exchanged[g, h, s] = start(len(exchanged), ref, place, other)
+            exchanged[g, h, s] = start(len(exchanged), 0, ref, place, other)
 
     def first(s, step):
         for h in range(2):
@@ -191,7 +190,7 @@
                 out1[h, step, s, c] = both(g, h, s, c).astype(BF16)
 
             n = 16 + 4 * s + 2 * step + h
-            firsts[h, s, step] = start(n, out1.at[h, step, s], in1.at[h, step, s], near[h])
+            firsts[h, s, step] = start(n, 1, out1.at[h, step, s], in1.at[h, step, s], near[h])
 
     def second(s):
         for h in range(2):
@@ -203,7 +202,7 @@
             def _(c):
                 out2[h, s, c] = (both(g, h, s, c) + in1[h, 0, s, c].astype(F32)).astype(BF16)
 
-            seconds[h, s] = start(24 + 2 * s + h, out2.at[h, s], in2.at[h, s], last[1 - h])
+            seconds[h, s] = start(24 + 2 * s + h, 2, out2.at[h, s], in2.at[h, s], last[1 - h])
 
     def own(s):
         for h in range(2):
@@ -220,22 +219,25 @@
         own(s)
         second(s)
     between(1)
-    for copy in (*exchanged.values(), *firsts.values()):
-        copy.wait_send()
+
+    def all_sent(kind, ref):
+        remote(ref, ref, sent_sems.at[kind], sems.at[0], other).wait_send()
+
+    all_sent(0, got)
+    all_sent(1, out1)
     for s in range(2):
         for h in range(2):
             seconds[h, s].wait_recv()
             finish(h, s, lambda c: in2[h, s, c].astype(F32))
-    for copy in seconds.values():
-        copy.wait_send()
+    all_sent(2, out2)
 
 
 def kernel(
     w1, w2, acts, act_mask, mask2, columns1, columns2, bias1_in, bias2_in, out,
     whole1, whole2, sums, x0, live, mask_own, mask_taken, masks2, columns_own, columns_in, bias1, bias2, table_v1, table_v2, table1, table2,
     out1, out2, got_a, in1_a, in2_a, got_b, in1_b, in2_b, kept, kept_out, kept_in,
-    load_sems, ring1_sems, ring2_sems, fetch_sems, mine_sems, taken_sems, small_sems, swap_sems, table_sems,
-    sems_a, sems_b, spread_sems, kept_sems,
+    load_sems, ring1_sems, ring2_sems, ring_sent, fetch_sems, mine_sem, taken_sems, small_sems, swap_sems, table_sems,
+    sems_a, sems_b, sent_a, sent_b, spread_sems, kept_sems,
 ):
     xh, core, y, z, xl = (lax.axis_index(a) for a in AXES)
     x = xh * 2 + xl
@@ -247,8 +249,8 @@
     near_y = ({"y": y + 1 - 2 * lax.rem(y, 2)}, {"y": 3 - y})
     last_y = tuple({**near, "core": xl, "xl": core} for near in near_y)
     beside = near_x[0]
-    ring1 = Ring(w1, whole1, z, load_sems, ring1_sems)
-    ring2 = Ring(w2, whole2, z, load_sems, ring2_sems)
+    ring1 = Ring(w1, whole1, z, load_sems, ring1_sems, ring_sent.at[0])
+    ring2 = Ring(w2, whole2, z, load_sems, ring2_sems, ring_sent.at[1])
 
     def rows_of(c):
         return pl.ds(pl.multiple_of(c * BS, BS), BS)
@@ -258,10 +260,10 @@
         return acts.at[:, pl.ds(pl.multiple_of(b * BS, BS), BS)]
 
     def given(i):
-        return remote(block(i, 1 - xl), x0.at[i, rows_of(xl)], taken_sems.at[0, i], taken_sems.at[1, i], beside)
+        return remote(block(i, 1 - xl), x0.at[i, rows_of(xl)], taken_sems.at[0], taken_sems.at[1], beside)
 
     def own(i):
-        return pltpu.make_async_copy(block(i, xl), x0.at[i, rows_of(xl)], mine_sems.at[i])
+        return pltpu.make_async_copy(block(i, xl), x0.at[i, rows_of(xl)], mine_sem)
 
     ring1.start_loads()
     greet((*ring1.to, other, home, *near_x, *near_y))
@@ -327,9 +329,9 @@
             factor = jnp.broadcast_to(column, (BS, BS)).astype(BF16)
             x0[i, rows, :] = x0[i, rows, :] * factor
 
-    @pl.loop(0, ORDER)
-    def _(i):
-        own(i).wait()
+    ref = x0.at[:, rows_of(xl)]
+    pltpu.make_async_copy(ref, ref, mine_sem).wait()
+    given_all = remote(ref, ref, taken_sems.at[0], taken_sems.at[1], beside)
 
     masked(mask_own, rows_of(xl))
     to_scalars1 = pltpu.make_async_copy(table_v1, table1, table_sems.at[0])
@@ -338,9 +340,7 @@
     for copy in small:
         copy.wait_recv()
 
-    @pl.loop(0, ORDER)
-    def _(i):
-        given(i).wait_recv()
+    given_all.wait_recv()
 
     masked(mask_taken, rows_of(1 - xl))
     to_scalars1.wait()
@@ -412,7 +412,7 @@
             spreads[h, s, to] = spread(x, h, s, to)
 
     reduce_scatter(
-        other, near_x, near_x, hidden_sum(core), hidden_sum(1 - core), sent, got_a, out1, in1_a, out2, in2_a, sems_a,
+        other, near_x, near_x, hidden_sum(core), hidden_sum(1 - core), sent, got_a, out1, in1_a, out2, in2_a, sems_a, sent_a,
         keep_hidden, finish_hidden, lambda stage: ring2.pumps(stage, stage + 1),
     )
     ring2.pumps(2, 4)
@@ -433,9 +433,7 @@
     use_arrived(x0, ring2, sums, table2, 0, 6, True)
     use_arrived(x0, ring2, sums, table2, 6, 10, False)
 
-    @pl.loop(0, ORDER)
-    def _(i):
-        given(i).wait_send()
+    given_all.wait_send()
 
     @pl.when(away)
     def _():
@@ -478,7 +476,7 @@
             out[:, n * BS : (n + 1) * BS] = jnp.maximum(total + bias2[pl.ds(n, 1), :], 0.0).astype(BF16)
 
     reduce_scatter(
-        other, near_y, last_y, result_sum(core), result_sum(1 - core), sent, got_b, out1, in1_b, out2, in2_b, sems_b,
+        other, near_y, last_y, result_sum(core), result_sum(1 - core), sent, got_b, out1, in1_b, out2, in2_b, sems_b, sent_b,
         keep_result, finish_result, lambda stage: None,
     )
 
@@ -532,16 +530,19 @@
             tiles(2, 2, PART),
             tiles(2, 2, PART),
             dma((CHUNKS,)),
-            dma((2, 2, HOPS)),
-            dma((2, 2, HOPS)),
+            dma((2, HOPS)),
+            dma((2, HOPS)),
+            dma((2,)),
             dma((5,)),
-            dma((ORDER,)),
-            dma((2, ORDER)),
+            dma(()),
+            dma((2,)),
             dma((2, 2)),
             dma((2, 2)),
             dma((2,)),
-            dma((2, 28)),
-            dma((2, 28)),
+            dma((28,)),
+            dma((28,)),
+            dma((3,)),
+            dma((3,)),
             dma((2, 12)),
             dma((2, 4)),
         ],

time: 197 us -> 195 us (0.990)
  Pallas kernels: 195 us -> 193 us
where the time goes in v7:
time: 195 us
  Pallas kernels  193 us (99%)
    pallas_call x1, Pallas kernels, on_device(): pl.pallas_call(kernel, out_shape=jax.ShapeDtypeStruct((n, UNITS * BS), BF...  193 us

profile of v7, /device:TPU:1, one launch (start us, length us, event | category | flops | bytes accessed | tf_op | source)
XLA Modules:
  0.0 194.7 jit_solution(592921079389524752)
XLA Ops:
  0.0 192.8 %layers.1 = bf16[128,2048]{1,0:T(8,128)(2,1)} custom-call(bf16[4,8,128,128]{3,2,1,0:T(8,128)(2,1)} %w1.1, bf16[4,8,128,128]{3,2,1,0:T(8,128)(2,1)} %w2.1, bf16[128,8192]{1,0:T(8,128)(2,1)} %acts.1, s32[64,128]{1,0:T(8,128)} %bitcast.6, s32[64,128]{1,0:T(8,128)} %bitcast.7, s32[8,64]{1,0:T(8,128)} %bitcast.10, s32[8,64]{1,0:T(8,128)} %bitcast.11, ...), custom_call_target="tpu_custom_call" | custom-call | tf_op jit(solution)/shard_map/layers/pallas_call | solution.py:503
  192.8 1.9 copy.11
